TPU v7x, 128 devices: a whole 4x4x4 slice. The times are simulated.
128 devices in a mesh: expert: 8 (over z, core), fsdp: 16 (over y, x).
Axes of the slice: x: 4, y: 4, z: 4, core: 2. Of those that a mesh axis runs over, the one named last changes fastest.
Arguments:
- hidden: bfloat16 [8, 768, 8192], P('expert', None, 'fsdp'), may hold values from -0.198873782 to 0.198873782
- expert_ids: int32 [2048, 2], P(('expert', 'fsdp')), may hold values from 0 to 7, all different within a row; in each aligned block of 16 rows (0 to 15, 16 to 31, ...) at most 6 rows name the same one
- gate_weights: float32 [2048, 2], P(('expert', 'fsdp')), may hold values from 0.2 to 1
- loss_weight: float32 [2048], P(('expert', 'fsdp')), may hold values from 0.3 to 3
- decay: float32 [1], replicated, may hold values from 0.2 to 0.6
- val_grad: bfloat16 [8, 8192, 4096], P('expert', 'fsdp'), may hold values from -8 to 8
- down_weight: bfloat16 [8, 8192, 4096], P('expert', 'fsdp'), may hold values from -0.0625 to 0.0625
Outputs:
- solution: float32 [8, 8192, 4096], P('expert', 'fsdp')
- hyper: float32 [1], replicated
Inputs may be any that keep to these rules, and one draw needn't show every extreme that they name: `expert_ids`: each token names 2 different experts; among the 16 tokens of one device no expert is named more than 6 times, a bound that some block reaches.
All inputs are finite; a program needn't handle non-finite values.
Results may differ from a plain program's by a relative error of at most 0.00067.
Values may be sent and summed in bfloat16 or wider, within the bound.
No kernel may reach another device: no remote copies, remote signals or barrier semaphores. Data moves between devices by JAX's collectives and lax.ppermute only.
A program may use at most 128 MiB of HBM per device.

v0:
```python
import math

import jax
import jax.numpy as jnp
from jax import lax
from jax.sharding import Mesh
from jax.sharding import PartitionSpec as P

D = 4096
ITERS = 2
EXPERT_FSDP = ("expert_0", "expert_1", "fsdp_0", "fsdp_1")
EXPERT = ("expert_0", "expert_1")
FSDP = ("fsdp_0", "fsdp_1")


def by_axis(array, axes):
    for axis in axes:
        array = lax.psum(array, axis)
    return array


def gate_table(expert_ids, gate_weights, experts, capacity):
    flat_ids = expert_ids.reshape(-1)
    labels = jnp.arange(experts, dtype=jnp.int32)
    onehot = (flat_ids[:, None] == labels[None, :]).astype(jnp.int32)
    earlier = jnp.cumsum(onehot, axis=0) - onehot
    slots = jnp.sum(earlier * onehot, axis=1)
    targets = flat_ids * capacity + slots
    columns = jnp.arange(experts * capacity, dtype=jnp.int32)
    hits = (targets[:, None] == columns[None, :]).astype(jnp.float32)
    weighted = hits * gate_weights.reshape(-1)[:, None]
    return jnp.sum(weighted.reshape(-1, expert_ids.shape[1], experts * capacity), axis=1)


def combine(table, weights, outputs):
    mixed = jnp.dot(
        table, outputs, precision=lax.Precision.HIGHEST, preferred_element_type=jnp.float32
    )
    scaled = weights[:, None] * mixed
    back = jnp.dot(
        table.T, scaled, precision=lax.Precision.HIGHEST, preferred_element_type=jnp.float32
    )
    return back.astype(jnp.bfloat16)


def joined_sums(residual, direction, image, target):
    return (
        by_axis(jnp.sum(residual * residual), EXPERT_FSDP),
        by_axis(jnp.sum(direction * image), EXPERT_FSDP),
        by_axis(jnp.sum(residual * image), EXPERT_FSDP),
        by_axis(jnp.sum(image * image), EXPERT_FSDP),
        by_axis(jnp.sum(target.astype(jnp.float32) * direction), EXPERT_FSDP),
    )


def local(hidden, expert_ids, gate_weights, loss_weight, decay, val_grad, down_weight):
    n_expert = lax.axis_size(EXPERT)
    n_fsdp = lax.axis_size(FSDP)
    capacity = hidden.shape[1] // (n_expert * n_fsdp)
    decay_rate = decay[0]
    table = gate_table(expert_ids, gate_weights, n_expert, capacity)
    local_hidden = hidden[0]
    right_side, target = (val_grad, down_weight)
    start_side = right_side.astype(jnp.float32)
    solution = jnp.zeros_like(start_side)
    residual = start_side
    direction = start_side
    along_total = jnp.float32(0.0)
    for iteration in range(ITERS):
        if iteration > 0:
            direction = residual + norm_guess / norm_prev * direction
        rounded = direction[0].astype(jnp.bfloat16)
        summed = lax.psum_scatter(
            jnp.dot(local_hidden, rounded, preferred_element_type=jnp.float32),
            FSDP,
            scatter_dimension=0,
            tiled=True,
        )
        arrived = lax.all_to_all(summed, EXPERT, split_axis=0, concat_axis=0, tiled=True)
        leaving = combine(table, loss_weight, arrived)
        returned = lax.all_to_all(leaving, EXPERT, split_axis=0, concat_axis=0, tiled=True)
        gradient = lax.dot_general(
            local_hidden,
            lax.all_gather(returned, FSDP, axis=0, tiled=True),
            (((0,), (0,)), ((), ())),
            preferred_element_type=jnp.float32,
        )
        image = gradient[None] + decay_rate * direction
        norm_now, curve, cross, square, along = joined_sums(residual, direction, image, target)
        alpha = norm_now / curve
        solution = solution + alpha * direction
        residual = residual - alpha * image
        norm_guess = norm_now - 2.0 * alpha * cross + alpha * alpha * square
        norm_prev = norm_now
        along_total = along_total + alpha * along
    hyper = -along_total / math.sqrt(n_expert * D)
    return (solution, jnp.reshape(hyper, (1,)))


def solution(mesh):
    finer = Mesh(mesh.devices.reshape(4, 2, 4, 4), ("expert_0", "expert_1", "fsdp_0", "fsdp_1"))
    placed = (
        P(EXPERT, None, FSDP),
        P(EXPERT_FSDP, None),
        P(EXPERT_FSDP, None),
        P(EXPERT_FSDP),
        P(),
        P(EXPERT, FSDP, None),
        P(EXPERT, FSDP, None),
    )
    return jax.shard_map(
        local, mesh=finer, in_specs=placed, out_specs=(P(EXPERT, FSDP, None), P()), check_vma=False
    )
```

profile of v0, /device:TPU:0, one launch (start us, length us, event | category | flops | bytes accessed | tf_op | source)
XLA Modules:
  0.0 544.2 jit_solution(16271983358100491739)
XLA Ops:
  7.2 1.1 copy-done
  8.3 8.6 %fusion.10 = f32[768,4096]{1,0:T(8,128)} fusion(bf16[1,512,4096]{2,1,0:T(8,128)(2,1)} %param.12, bf16[1,768,512]{2,1,0:T(8,128)(2,1)S(1)} %copy-done), kind=kOutput, calls=%fused_computation.26 | convolution fusion | flops 3221225472 | bytes 17563648 | tf_op jit(solution)/shard_map/dot_general | solution.py:74
  16.9 97.7 %reduce-scatter.5.cloned.1.call-done = f32[48,4096]{1,0:T(8,128)} async-done(((f32[768,4096]{1,0:T(8,128)}), f32[48,4096]{1,0:T(8,128)}) %reduce-scatter.5.cloned.1.call-update) | async-done | bytes 786448 | tf_op jit(solution)/shard_map/reduce_scatter | solution.py:73
  114.5 2.2 all_to_all.32
  116.7 4.4 all-to-all-start
  122.0 15.1 %all-to-all-done = f32[8,6,4096]{2,1,0:T(8,128)S(1)} async-done(((f32[8,6,4096]{2,1,0:T(8,128)}), f32[8,6,4096]{2,1,0:T(8,128)S(1)}, u32[]{:S(2)}, u32[]{:S(2)}) %all-to-all-start) | async-done | bytes 786464 | tf_op jit(solution)/shard_map/all_to_all | solution.py:79
  138.7 12.8 %all_to_all.48 = bf16[8,6,4096]{2,1,0:T(8,128)(2,1)S(1)} all-to-all(bf16[8,6,4096]{2,1,0:T(8,128)(2,1)S(1)} %all_to_all.35), channel_id=1, replica_groups=mesh['expert_0'=4,'expert_1'=2,'fsdp_0'=4,'fsdp_1'=4] {'expert_0','exper..., dimensions={0} | all-to-all | bytes 786432 | tf_op jit(solution)/shard_map/all_to_all | solution.py:81
  151.5 0.9 all_to_all.37
  152.4 6.5 %copy.40 = bf16[1,512,4096]{1,2,0:T(8,128)(2,1)} copy(bf16[1,512,4096]{2,1,0:T(8,128)(2,1)} %param.12) | data formatting | bytes 8388608 | tf_op args[5]
  159.6 51.1 %all-gather.3.cloned.1.call-done = bf16[768,4096]{1,0:T(8,128)(2,1)} async-done(((bf16[48,4096]{1,0:T(8,128)(2,1)}), bf16[768,4096]{1,0:T(8,128)(2,1)}) %all-gather.3.cloned.1.call-update) | async-done | bytes 6291472 | tf_op jit(solution)/shard_map/all_gather | solution.py:84
  210.7 12.3 %multiply_reduce_fusion = (f32[]{:T(128)}, f32[]{:T(128)}, f32[]{:T(128)}, f32[1,512,4096]{1,2,0:T(8,128)}) fusion(bf16[1,512,4096]{1,2,0:T(8,128)(2,1)} %copy.40, f32[]{:T(128)} %bitcast.44, bf16[768,4096]{1,0:T(8,128)(2,1)} %all-gather.3.cloned.1.call-done, bf16[1,768,512]{2,1,0:T(8,128)(2,1)S(1)} %copy-done), kind=kOutput, calls=%fused_computation.18 | convolution fusion | flops 3240099840 | bytes 19660816 | tf_op jit(solution)/shard_map/dot_general | solution.py:82
  222.9 11.4 %all-reduce.5 = (f32[]{:T(128)}, f32[]{:T(128)}, f32[]{:T(128)}) all-reduce(f32[]{:T(128)} %get-tuple-element.17, f32[]{:T(128)} %get-tuple-element.16, f32[]{:T(128)} %get-tuple-element.15), channel_id=1, replica_groups=mesh['expert_0'=4,'expert_1'=2,'fsdp_0'=4,'fsdp_1'=4] {'expert_0'}, use_global_device_ids=true, to_apply=%region_1.2 | all-reduce | flops 3 | bytes 24 | tf_op jit(solution)/shard_map/psum | solution.py:18
  234.3 3.1 all-reduce.7
  237.4 11.1 %all-reduce.3 = (f32[]{:T(128)}, f32[]{:T(128)}, f32[]{:T(128)}) all-reduce(f32[]{:T(128)} %get-tuple-element.43, f32[]{:T(128)} %get-tuple-element.44, f32[]{:T(128)} %get-tuple-element.45), channel_id=1, replica_groups=mesh['expert_0'=4,'expert_1'=2,'fsdp_0'=4,'fsdp_1'=4] {'fsdp_0'}, use_global_device_ids=true, to_apply=%region_3.4 | all-reduce | flops 3 | bytes 24 | tf_op jit(solution)/shard_map/psum | solution.py:18
  248.5 9.4 %all-reduce.1 = (f32[]{:T(128)}, f32[]{:T(128)}, f32[]{:T(128)}) all-reduce(f32[]{:T(128)} %get-tuple-element.29, f32[]{:T(128)} %get-tuple-element.30, f32[]{:T(128)} %get-tuple-element.31), channel_id=1, replica_groups=mesh['expert_0'=4,'expert_1'=2,'fsdp_0'=4,'fsdp_1'=4] {'fsdp_1'}, use_global_device_ids=true, to_apply=%region_4.5 | all-reduce | flops 3 | bytes 24 | tf_op jit(solution)/shard_map/psum | solution.py:18
  261.8 13.1 %convolution_bitcast_fusion = f32[768,4096]{0,1:T(8,128)} fusion(bf16[1,768,512]{2,1,0:T(8,128)(2,1)S(1)} %copy-done, bf16[1,512,4096]{1,2,0:T(8,128)(2,1)} %copy.40, f32[1,512,4096]{1,2,0:T(8,128)} %get-tuple-element.46, f32[]{:T(128)S(6)} %div.13, f32[]{:T(128)S(6)} %div.12), kind=kOutput, calls=%fused_computation.20 | convolution fusion | flops 3233808384 | bytes 25952264 | tf_op jit(solution)/shard_map/dot_general | solution.py:74
  274.9 12.6 %copy.46 = f32[768,4096]{1,0:T(8,128)} copy(f32[768,4096]{0,1:T(8,128)} %convolution_bitcast_fusion) | data formatting | bytes 25165824
  287.6 89.8 %reduce-scatter.7.cloned.1.call-done = f32[48,4096]{1,0:T(8,128)} async-done(((f32[768,4096]{1,0:T(8,128)}), f32[48,4096]{1,0:T(8,128)}) %reduce-scatter.7.cloned.1.call-update) | async-done | bytes 786448 | tf_op jit(solution)/shard_map/reduce_scatter | solution.py:73
  377.4 1.2 all_to_all.38
  378.6 20.2 %all_to_all.49 = f32[8,6,4096]{2,1,0:T(8,128)S(1)} all-to-all(f32[8,6,4096]{2,1,0:T(8,128)S(1)} %all_to_all.38), channel_id=1, replica_groups=mesh['expert_0'=4,'expert_1'=2,'fsdp_0'=4,'fsdp_1'=4] {'expert_0','exper..., dimensions={0} | all-to-all | bytes 1572864 | tf_op jit(solution)/shard_map/all_to_all | solution.py:79
  400.4 12.8 %all_to_all.50 = bf16[8,6,4096]{2,1,0:T(8,128)(2,1)S(1)} all-to-all(bf16[8,6,4096]{2,1,0:T(8,128)(2,1)S(1)} %all_to_all.41), channel_id=1, replica_groups=mesh['expert_0'=4,'expert_1'=2,'fsdp_0'=4,'fsdp_1'=4] {'expert_0','exper..., dimensions={0} | all-to-all | bytes 786432 | tf_op jit(solution)/shard_map/all_to_all | solution.py:81
  413.1 0.9 all_to_all.43
  414.1 6.6 %copy.44 = bf16[1,512,4096]{1,2,0:T(8,128)(2,1)} copy(bf16[1,512,4096]{2,1,0:T(8,128)(2,1)} %param.13) | data formatting | bytes 8388608 | tf_op args[6]
  420.7 8.4 %fusion = (f32[]{:T(128)}, f32[]{:T(128)}, f32[]{:T(128)}) fusion(bf16[1,512,4096]{1,2,0:T(8,128)(2,1)} %copy.44, f32[]{:T(128)S(6)} %div.13, f32[1,512,4096]{1,2,0:T(8,128)} %get-tuple-element.46, f32[]{:T(128)S(6)} %div.12, bf16[1,512,4096]{1,2,0:T(8,128)(2,1)} %copy.40), kind=kLoop, calls=%fused_computation.8 | loop fusion | flops 25165824 | bytes 16777236 | tf_op jit(solution)/shard_map/reduce_sum | solution.py:52
  429.0 43.4 %all-gather.5.cloned.1.call-done = bf16[768,4096]{1,0:T(8,128)(2,1)} async-done(((bf16[48,4096]{1,0:T(8,128)(2,1)}), bf16[768,4096]{1,0:T(8,128)(2,1)}) %all-gather.5.cloned.1.call-update) | async-done | bytes 6291472 | tf_op jit(solution)/shard_map/all_gather | solution.py:84
  472.4 10.1 %fusion.8 = f32[]{:T(128)} fusion(bf16[768,4096]{1,0:T(8,128)(2,1)} %all-gather.5.cloned.1.call-done, f32[]{:T(128)} %bitcast.45, bf16[1,768,512]{2,1,0:T(8,128)(2,1)S(1)} %copy-done, f32[]{:T(128)S(6)} %div.13, f32[1,512,4096]{1,2,0:T(8,128)} %get-tuple-element.46, f32[]{:T(128)S(6)} %div.12, bf16[1,512,4096]{1,2,0:T(8,128)(2,1)} %copy.40), kind=kOutput, calls=%fused_computation.17 | convolution fusion | flops 3240099840 | bytes 19660816 | tf_op jit(solution)/shard_map/dot_general | solution.py:82
  482.5 11.4 %all-reduce.4 = (f32[]{:T(128)}, f32[]{:T(128)}, f32[]{:T(128)}, f32[]{:T(128)}) all-reduce(f32[]{:T(128)} %get-tuple-element.13, f32[]{:T(128)} %fusion.8, f32[]{:T(128)} %get-tuple-element.14, f32[]{:T(128)} %get-tuple-element.12), channel_id=1, replica_groups=mesh['expert_0'=4,'expert_1'=2,'fsdp_0'=4,'fsdp_1'=4] {'expert_0'}, use_global_device_ids=true, to_apply=%region_15.16 | all-reduce | flops 4 | bytes 32 | tf_op jit(solution)/shard_map/psum | solution.py:18
  493.9 3.2 all-reduce.6
  497.0 11.1 %all-reduce.2 = (f32[]{:T(128)}, f32[]{:T(128)}, f32[]{:T(128)}, f32[]{:T(128)}) all-reduce(f32[]{:T(128)} %get-tuple-element.39, f32[]{:T(128)} %get-tuple-element.40, f32[]{:T(128)} %get-tuple-element.41, f32[]{:T(128)} %get-tuple-element.42), channel_id=1, replica_groups=mesh['expert_0'=4,'expert_1'=2,'fsdp_0'=4,'fsdp_1'=4] {'fsdp_0'}, use_global_device_ids=true, to_apply=%region_17.18 | all-reduce | flops 4 | bytes 32 | tf_op jit(solution)/shard_map/psum | solution.py:18
  508.1 9.2 %all-reduce = (f32[]{:T(128)}, f32[]{:T(128)}, f32[]{:T(128)}, f32[]{:T(128)}) all-reduce(f32[]{:T(128)} %get-tuple-element.25, f32[]{:T(128)} %get-tuple-element.26, f32[]{:T(128)} %get-tuple-element.27, f32[]{:T(128)} %get-tuple-element.28), channel_id=1, replica_groups=mesh['expert_0'=4,'expert_1'=2,'fsdp_0'=4,'fsdp_1'=4] {'fsdp_1'}, use_global_device_ids=true, to_apply=%region_18.19 | all-reduce | flops 4 | bytes 32 | tf_op jit(solution)/shard_map/psum | solution.py:18
  518.7 7.7 %fusion.4 = f32[1,512,4096]{1,2,0:T(8,128)} fusion(bf16[1,512,4096]{1,2,0:T(8,128)(2,1)} %copy.40, f32[]{:T(128)S(6)} %div.14, f32[]{:T(128)S(6)} %div.12, f32[]{:T(128)S(6)} %div.13, f32[1,512,4096]{1,2,0:T(8,128)} %get-tuple-element.46), kind=kLoop, calls=%fused_computation.12 | loop fusion | flops 16777216 | bytes 20971532 | tf_op jit(solution)/shard_map/add | solution.py:91
  527.6 8.9 %copy.45 = f32[1,512,4096]{2,1,0:T(8,128)} copy(f32[1,512,4096]{1,2,0:T(8,128)} %fusion.4) | data formatting | bytes 16777216
  (32 shorter events, 4.1 us)
Async XLA Ops:
  7.2 1.1 copy-start
  7.2 107.4 %reduce-scatter.5.cloned.1.call-start = ((), (), s32[]{:S(2)}) async-start(), calls=%async_computation.6 | async-start | bytes 13369344 | tf_op jit(solution)/shard_map/reduce_scatter | solution.py:73
  16.9 104.4 %copy-start.1 = (s32[16,2]{0,1:T(2,128)S(1)}, s32[16,2]{0,1:T(2,128)}, u32[]{:S(2)}) copy-start(s32[16,2]{0,1:T(2,128)} %param.8) | copy-start | bytes 388
  16.9 105.0 %copy-start.3 = (f32[16,2]{0,1:T(2,128)S(1)}, f32[16,2]{0,1:T(2,128)}, u32[]{:S(2)}) copy-start(f32[16,2]{0,1:T(2,128)} %param.9) | copy-start | bytes 388
  16.9 120.4 %copy-start.2 = (f32[16]{0:T(128)S(1)}, f32[16]{0:T(128)}, u32[]{:S(2)}) copy-start(f32[16]{0:T(128)} %param.10) | copy-start | bytes 196
  116.7 20.4 %all-to-all-start = ((f32[8,6,4096]{2,1,0:T(8,128)}), f32[8,6,4096]{2,1,0:T(8,128)S(1)}, u32[]{:S(2)}, u32[]{:S(2)}) async-start(f32[8,6,4096]{2,1,0:T(8,128)} %all_to_all.32), calls=%async_computation.1 | async-start | bytes 2097152 | tf_op jit(solution)/shard_map/all_to_all | solution.py:79
  121.2 89.5 %all-gather.3.cloned.1.call-start = ((), (), s32[]{:S(2)}) async-start(), calls=%async_computation.7 | async-start | bytes 6684672 | tf_op jit(solution)/shard_map/all_gather | solution.py:84
  152.4 225.0 %reduce-scatter.7.cloned.1.call-start = ((), (), s32[]{:S(2)}) async-start(), calls=%async_computation.9 | async-start | bytes 13369344 | tf_op jit(solution)/shard_map/reduce_scatter | solution.py:73
  287.5 184.9 %all-gather.5.cloned.1.call-start = ((), (), s32[]{:S(2)}) async-start(), calls=%async_computation.8 | async-start | bytes 6684672 | tf_op jit(solution)/shard_map/all_gather | solution.py:84
Sparse Core Ops, SparseCore 0:
  17.0 97.4 reduce-scatter.4
  152.5 58.1 all-gather.2
  287.6 89.6 reduce-scatter.6
  414.2 58.1 all-gather.4
where the time goes:
time: 545 us; the launch traced here: 544 us
  waiting for transfers between devices  297 us (54%)
  blocking collectives  116 us (21%)
  matrix products  46.6 us (9%)
  local copies, waits for them, and re-layouts  41.8 us (8%)
  between operations  22 us (4%)
  other arithmetic  16.5 us (3%)
    reduce_scatter x2, waiting for transfers between devices, local(): lax.psum_scatter(jnp.dot(local_hidden, rounded, preferred_element_type=jn...  187 us
    all_gather x2, waiting for transfers between devices, local(): lax.all_gather(returned, FSDP, axis=0, tiled=True)  94.5 us
    psum x8, blocking collectives, by_axis(): array = lax.psum(array, axis)  69.9 us
    unnamed x13, local copies, waits for them, and re-layouts  35.8 us
    all_to_all x2, blocking collectives, local(): lax.all_to_all(leaving, EXPERT, split_axis=0, concat_axis=0, tiled=True)  25.5 us
    dot_general x2, matrix products, local(): lax.dot_general(local_hidden, lax.all_gather(returned, FSDP, axis=0, tile...  22.3 us
    dot_general x2, matrix products, local(): jnp.dot(local_hidden, rounded, preferred_element_type=jnp.float32)  21.6 us
    all_to_all x1, blocking collectives, local(): lax.all_to_all(summed, EXPERT, split_axis=0, concat_axis=0, tiled=True)  20.2 us
  transfers between devices with their start and end apart: 5, of which 5 were waited for; matrix products, arithmetic and copies ran while one was open for 4% of the time, Pallas kernels for 0%

commit v1 on v0

v1 whole, which is shorter than its diff:
```python
import functools
import math

import jax
import jax.numpy as jnp
from jax import lax
from jax.experimental import pallas as pl
from jax.experimental.pallas import tpu as pltpu
from jax.sharding import Mesh
from jax.sharding import PartitionSpec as P

EXPERT_FSDP = ("expert_0", "expert_1", "fsdp_0", "fsdp_1")
EXPERT = ("expert_0", "expert_1")
FSDP = ("fsdp_0", "fsdp_1")
PARAMS = dict(vmem_limit_bytes=48 * 1024 * 1024)


def shift(array, axis, amount):
    size = lax.axis_size(axis)
    return lax.ppermute(array, axis, [(i, (i + amount) % size) for i in range(size)])


def pick(array, index):
    return lax.dynamic_index_in_dim(array, index, 0, keepdims=False)


def exchange_axis(blocks, axis):
    size = lax.axis_size(axis)
    me = lax.axis_index(axis)
    received = [(me, pick(blocks, me))]
    for step in range(1, size):
        sent = pick(blocks, (me + step) % size)
        received.append(((me - step) % size, shift(sent, axis, step)))
    return received


def placed(received, size):
    first = received[0][1]
    array = jnp.zeros((size,) + first.shape, first.dtype)
    for index, block in received:
        array = lax.dynamic_update_index_in_dim(array, block, index, 0)
    return array


def gather_axis(block, axis):
    size = lax.axis_size(axis)
    me = lax.axis_index(axis)
    received = [(me, block)]
    for step in range(1, size):
        received.append(((me - step) % size, shift(block, axis, step)))
    return placed(received, size)


def expert_exchange(rows):
    outer, inner = lax.axis_size("expert_0"), lax.axis_size("expert_1")
    block = rows.shape[0] // (outer * inner)
    blocks = rows.reshape((outer, inner, block) + rows.shape[1:]).swapaxes(0, 1)
    by_core = placed(exchange_axis(blocks, "expert_1"), inner)
    by_chip = placed(exchange_axis(by_core.swapaxes(0, 1), "expert_0"), outer)
    return by_chip.reshape(rows.shape)


def gram(hidden):
    partial = lax.dot_general(
        hidden, hidden, (((1,), (1,)), ((), ())), preferred_element_type=jnp.float32
    )
    size = partial.shape[0]
    block = partial
    for axis in FSDP:
        parts = lax.axis_size(axis)
        block = block.reshape(parts, -1, size).astype(jnp.bfloat16)
        terms = exchange_axis(block, axis)
        block = sum(term.astype(jnp.float32) for _, term in terms)
    block = block.astype(jnp.bfloat16)
    for axis in FSDP[::-1]:
        block = gather_axis(block, axis).reshape(-1, size)
    return block


def all_sum(values):
    for axis in EXPERT_FSDP[::-1]:
        size = lax.axis_size(axis)
        values = sum([values] + [shift(values, axis, step) for step in range(1, size)])
    return values


def gate_tables(packed, experts, capacity):
    blocks, tokens, _ = packed.shape
    top = (packed.shape[2] - 1) // 2
    ids = packed[:, :, :top].reshape(blocks, tokens * top).astype(jnp.int32)
    gates = packed[:, :, top : 2 * top].reshape(blocks, tokens * top)
    same = ids[:, :, None] == ids[:, None, :]
    order = jnp.arange(tokens * top)
    earlier = order[None, :] < order[:, None]
    slots = jnp.sum((same & earlier[None]).astype(jnp.int32), axis=2)
    column = ids * (blocks * capacity) + jnp.arange(blocks)[:, None] * capacity + slots
    columns = jnp.arange(experts * blocks * capacity)
    hits = column[:, :, None] == columns[None, None, :]
    weighted = jnp.where(hits, gates[:, :, None], 0.0)
    weighted = weighted.reshape(blocks * tokens, top, -1)
    return jnp.sum(weighted, axis=1), packed[:, :, 2 * top].reshape(-1)


def outputs_kernel(hidden_ref, side_ref, out_ref):
    out_ref[0] = jnp.dot(hidden_ref[...], side_ref[...], preferred_element_type=jnp.float32)


def expert_outputs(hidden, side, parts):
    rows, depth = hidden.shape
    width = side.shape[1] // parts
    return pl.pallas_call(
        outputs_kernel,
        grid=(parts,),
        in_specs=[
            pl.BlockSpec((rows, depth), lambda i: (0, 0)),
            pl.BlockSpec((depth, width), lambda i: (0, i)),
        ],
        out_specs=pl.BlockSpec((1, rows, width), lambda i: (i, 0, 0)),
        out_shape=jax.ShapeDtypeStruct((parts, rows, width), jnp.float32),
        compiler_params=pltpu.CompilerParams(**PARAMS),
        cost_estimate=pl.CostEstimate(
            flops=2 * rows * depth * side.shape[1],
            bytes_accessed=4 * rows * side.shape[1],
            transcendentals=0,
        ),
        name="expert_outputs",
    )(hidden, side)


def finish_kernel(coef_ref, hidden_ref, tangent_ref, side_ref, target_ref, out_ref, along_ref):
    image = jnp.dot(hidden_ref[...], tangent_ref[0], preferred_element_type=jnp.float32)
    side = side_ref[...].astype(jnp.float32)
    out_ref[...] = coef_ref[0] * side + coef_ref[1] * image
    product = target_ref[...].astype(jnp.float32) * image
    along_ref[0] = jnp.sum(product.reshape(-1, 8, product.shape[1]), axis=0)


def finish(coefs, hidden_t, tangents, side, target):
    parts, rows, width = tangents.shape
    depth = hidden_t.shape[0]
    return pl.pallas_call(
        finish_kernel,
        grid=(parts,),
        in_specs=[
            pl.BlockSpec(memory_space=pltpu.SMEM),
            pl.BlockSpec((depth, rows), lambda i: (0, 0)),
            pl.BlockSpec((1, rows, width), lambda i: (i, 0, 0)),
            pl.BlockSpec((depth, width), lambda i: (0, i)),
            pl.BlockSpec((depth, width), lambda i: (0, i)),
        ],
        out_specs=[
            pl.BlockSpec((depth, width), lambda i: (0, i)),
            pl.BlockSpec((1, 8, width), lambda i: (i, 0, 0)),
        ],
        out_shape=[
            jax.ShapeDtypeStruct((depth, parts * width), jnp.float32),
            jax.ShapeDtypeStruct((parts, 8, width), jnp.float32),
        ],
        compiler_params=pltpu.CompilerParams(**PARAMS),
        cost_estimate=pl.CostEstimate(
            flops=2 * rows * depth * parts * width,
            bytes_accessed=10 * depth * parts * width,
            transcendentals=0,
        ),
        name="finish",
    )(coefs, hidden_t, tangents, side, target)


def mix(table, rows):
    return jnp.dot(
        table, rows, precision=lax.Precision.HIGHEST, preferred_element_type=jnp.float32
    )


def local(hidden, expert_ids, gate_weights, loss_weight, decay, val_grad, down_weight):
    n_expert = lax.axis_size(EXPERT)
    n_fsdp = lax.axis_size(FSDP)
    capacity = hidden.shape[1] // (n_expert * n_fsdp)
    tokens, top = expert_ids.shape
    rate = decay[0]
    acts, side, target = hidden[0], val_grad[0], down_weight[0]

    partial = expert_outputs(acts, side, n_fsdp)
    rows, width = partial.shape[1:]
    summed = lax.psum_scatter(
        partial.reshape(n_fsdp * rows, width), FSDP, scatter_dimension=0, tiled=True
    )

    packed = jnp.concatenate(
        [expert_ids.astype(jnp.float32), gate_weights, loss_weight[:, None]], axis=1
    )
    share = n_fsdp // n_expert
    everyone = lax.all_gather(packed, EXPERT_FSDP).reshape(n_expert, n_fsdp, tokens, -1)
    mine = lax.dynamic_slice_in_dim(everyone, lax.axis_index(EXPERT) * share, share, 1)
    mine = mine.swapaxes(0, 1).reshape(share * n_expert, tokens, -1)
    table, weights = gate_tables(mine, n_expert, capacity)
    kernel_matrix = gram(acts)
    wide = side.astype(jnp.float32)
    norm = jnp.sum(wide * wide)
    fixed = jnp.sum(target.astype(jnp.float32) * wide)

    arrived = expert_exchange(summed)
    mixed = mix(table, arrived)
    scaled = weights[:, None] * mixed
    leaving = mix(table.T, scaled).astype(jnp.bfloat16)
    returned = expert_exchange(leaving)
    tangents = lax.all_gather(returned, FSDP, axis=0, tiled=True)

    second = jnp.dot(kernel_matrix, returned, preferred_element_type=jnp.float32)
    square = jnp.sum(second * returned.astype(jnp.float32))
    again = mix(table, expert_exchange(second.astype(jnp.bfloat16)).astype(jnp.float32))
    parts = jnp.stack(
        [
            norm,
            jnp.sum(scaled * mixed),
            square,
            jnp.sum(weights[:, None] * again * again),
            fixed,
        ]
    )
    bb, bg, gg, ghg, wb = all_sum(parts)
    alpha = bb / (bg + rate * bb)
    lean = bg / bb
    across = gg - bg * lean
    fresh = alpha * alpha * across
    beta = fresh / bb
    bent = ghg - 2.0 * lean * gg + lean * lean * bg
    curve = alpha * alpha * (bent + rate * across) - beta * fresh / alpha
    step = fresh / curve
    keep = alpha + step * (beta + alpha * lean)
    move = -step * alpha

    result, along = finish(
        jnp.stack([keep, move]), acts.T, tangents.reshape(n_fsdp, rows, width), side, target
    )
    wg = all_sum(jnp.sum(along).reshape(1))[0]
    hyper = -(keep * wb + move * wg) / math.sqrt(n_expert * side.shape[1])
    return (result[None], jnp.reshape(hyper, (1,)))


def solution(mesh):
    finer = Mesh(mesh.devices.reshape(4, 2, 4, 4), EXPERT_FSDP)
    specs = (
        P(EXPERT, None, FSDP),
        P(EXPERT_FSDP, None),
        P(EXPERT_FSDP, None),
        P(EXPERT_FSDP),
        P(),
        P(EXPERT, FSDP, None),
        P(EXPERT, FSDP, None),
    )
    return jax.shard_map(
        local, mesh=finer, in_specs=specs, out_specs=(P(EXPERT, FSDP, None), P()), check_vma=False
    )
```

time: 545 us -> 333 us (0.61)
  waiting for transfers between devices: 297 us -> 116 us
  starting transfers between devices: 4.58 us -> 69.9 us
  blocking collectives: 116 us -> 61.3 us
  matrix products: 46.6 us -> 5.39 us
  local copies, waits for them, and re-layouts: 41.8 us -> 14.7 us
  Pallas kernels: 0 us -> 25.6 us
  between operations: 22 us -> 31.4 us
  other arithmetic: 16.5 us -> 8.27 us
    reduce_scatter x2 -> x1, waiting for transfers between devices: 187 us -> 34.9 us  [local(): lax.psum_scatter(partial.reshape(n_fsdp * rows, width), FSDP, scatter_dim...]
    all_gather x2 -> x1, waiting for transfers between devices: 94.5 us -> 0.01 us  [local(): tangents = lax.all_gather(returned, FSDP, axis=0, tiled=True)]
    ppermute x0 -> x44, waiting for transfers between devices: none -> 80.6 us  [shift(): lax.ppermute(array, axis, [(i, (i + amount) % size) for i in range(size)])]
    psum x8 -> x0, blocking collectives: 69.9 us -> none  [by_axis(): array = lax.psum(array, axis)]
    ppermute x0 -> x44, starting transfers between devices: none -> 69.8 us  [shift(): lax.ppermute(array, axis, [(i, (i + amount) % size) for i in range(size)])]
    all_gather x0 -> x1, blocking collectives: none -> 61.3 us  [local(): lax.all_gather(packed, EXPERT_FSDP).reshape(n_expert, n_fsdp, tokens, -1)]
    all_to_all x3 -> x0, blocking collectives: 45.7 us -> none  [the longest x2 25.5 us: local(): lax.all_to_all(leaving, EXPERT, split_axis=0, concat_axis=0, tiled=True)]
    dot_general x8 -> x5, matrix products: 46.6 us -> 5.39 us  [the longest x3 3.46 us: mix(): jnp.dot(table, rows, precision=lax.Precision.HIGHEST, preferred_element_t...]
  transfers between devices with their start and end apart: 5 -> 46, of which waited for: 5 -> 36; matrix products, arithmetic and copies ran while one was open for 4% -> 5% of each run, Pallas kernels for 0% -> 0%
where the time goes in v1:
time: 333 us; the launch traced here: 332 us
  waiting for transfers between devices  116 us (35%)
  starting transfers between devices  69.9 us (21%)
  blocking collectives  61.3 us (18%)
  between operations  31.4 us (9%)
  Pallas kernels  25.6 us (8%)
  local copies, waits for them, and re-layouts  14.7 us (4%)
  other arithmetic  8.27 us (2%)
  matrix products  5.39 us (2%)
    ppermute x44, waiting for transfers between devices, shift(): lax.ppermute(array, axis, [(i, (i + amount) % size) for i in range(size)])  80.6 us
    ppermute x44, starting transfers between devices, shift(): lax.ppermute(array, axis, [(i, (i + amount) % size) for i in range(size)])  69.8 us
    all_gather x1, blocking collectives, local(): lax.all_gather(packed, EXPERT_FSDP).reshape(n_expert, n_fsdp, tokens, -1)  61.3 us
    reduce_scatter x1, waiting for transfers between devices, local(): lax.psum_scatter(partial.reshape(n_fsdp * rows, width), FSDP, scatter_dim...  34.9 us
    pallas_call x1, Pallas kernels, finish(): pl.pallas_call(finish_kernel, grid=(parts,), in_specs=[pl.BlockSpec(memor...  14.7 us
    pallas_call x1, Pallas kernels, expert_outputs(): pl.pallas_call(outputs_kernel, grid=(parts,), in_specs=[pl.BlockSpec((row...  10.9 us
    unnamed x23, local copies, waits for them, and re-layouts  7.13 us
  transfers between devices with their start and end apart: 46, of which 36 were waited for; matrix products, arithmetic and copies ran while one was open for 5% of the time, Pallas kernels for 0%

profile of v1, /device:TPU:0, one launch (start us, length us, event | category | flops | bytes accessed | tf_op | source)
XLA Modules:
  0.0 332.1 jit_solution(3584577247409986873)
XLA Ops:
  7.2 2.2 copy-done
  10.5 10.9 %expert_outputs.1 = f32[16,768,256]{2,1,0:T(8,128)} custom-call(bf16[768,512]{1,0:T(8,128)(2,1)S(1)} %bitcast.168, bf16[512,4096]{1,0:T(8,128)(2,1)S(1)} %bitcast.166), custom_call_target="tpu_custom_call" | custom-call | flops 3221225472 | bytes 12582912 | tf_op jit(solution)/shard_map/expert_outputs/pallas_call | solution.py:111
  22.2 61.3 %all-gather.1 = f32[128,16,5]{1,2,0:T(8,128)S(1)} all-gather(f32[1,16,5]{1,2,0:T(8,128)S(1)} %maximum_bitcast_fusion), channel_id=2, replica_groups=mesh['expert_0'=4,'expert_1'=2,'fsdp_0'=4,'fsdp_1'=4] {'expert_0','exper..., dimensions={0}, use_global_device_ids=true | all-gather | bytes 41280 | tf_op jit(solution)/shard_map/all_gather | solution.py:193
  84.1 34.9 %reduce-scatter.2.cloned.1.call-done = f32[768,256]{1,0:T(8,128)} async-done(((f32[12288,256]{1,0:T(8,128)}), f32[768,256]{1,0:T(8,128)}) %reduce-scatter.2.cloned.1.call-update) | async-done | bytes 786448 | tf_op jit(solution)/shard_map/reduce_scatter | solution.py:185
  123.9 3.0 collective-permute-start.2
  128.3 2.0 collective-permute-done.1
  130.3 5.4 %collective-permute-done.2 = f32[2,96,256]{2,1,0:T(8,128)S(1)} collective-permute-done((f32[2,96,256]{2,1,0:T(8,128)S(1)}, f32[2,96,256]{2,1,0:T(8,128)S(1)}, u32[]{:S(2)}, u32[]{:S(2)}) %collective-permute-start.2) | collective-permute-done | bytes 196640 | tf_op jit(solution)/shard_map/ppermute | solution.py:20
  141.1 2.4 collective-permute-start.18
  146.0 2.4 collective-permute-done.18
  152.1 2.3 collective-permute-start.5
  155.9 6.4 %collective-permute-done.4 = bf16[192,768]{1,0:T(8,128)(2,1)} collective-permute-done((bf16[192,768]{1,0:T(8,128)(2,1)}, bf16[192,768]{1,0:T(8,128)(2,1)}, u32[]{:S(2)}, u32[]{:S(2)}) %collective-permute-start.4) | collective-permute-done | bytes 294944 | tf_op jit(solution)/shard_map/ppermute | solution.py:20
  162.4 10.1 %collective-permute-done.5 = bf16[192,768]{1,0:T(8,128)(2,1)} collective-permute-done((bf16[192,768]{1,0:T(8,128)(2,1)}, bf16[192,768]{1,0:T(8,128)(2,1)}, u32[]{:S(2)}, u32[]{:S(2)}) %collective-permute-start.5) | collective-permute-done | bytes 294944 | tf_op jit(solution)/shard_map/ppermute | solution.py:20
  183.8 3.0 collective-permute-start.11
  187.0 2.5 collective-permute-done.10
  189.5 3.6 %collective-permute-done.11 = bf16[48,768]{1,0:T(8,128)(2,1)S(1)} collective-permute-done((bf16[48,768]{1,0:T(8,128)(2,1)S(1)}, bf16[48,768]{1,0:T(8,128)(2,1)S(1)}, u32[]{:S(2)}, u32[]{:S(2)}) %collective-permute-start.11) | collective-permute-done | bytes 73760 | tf_op jit(solution)/shard_map/ppermute | solution.py:20
  194.5 3.2 collective-permute-start.14
  198.2 12.0 %collective-permute-done.13 = bf16[192,768]{1,0:T(8,128)(2,1)S(1)} collective-permute-done((bf16[192,768]{1,0:T(8,128)(2,1)S(1)}, bf16[192,768]{1,0:T(8,128)(2,1)S(1)}, u32[]{:S(2)}, u32[]{:S(2)}) %collective-permute-start.13) | collective-permute-done | bytes 294944 | tf_op jit(solution)/shard_map/ppermute | solution.py:20
  210.3 13.2 %collective-permute-done.14 = bf16[192,768]{1,0:T(8,128)(2,1)S(1)} collective-permute-done((bf16[192,768]{1,0:T(8,128)(2,1)S(1)}, bf16[192,768]{1,0:T(8,128)(2,1)S(1)}, u32[]{:S(2)}, u32[]{:S(2)}) %collective-permute-start.14) | collective-permute-done | bytes 294944 | tf_op jit(solution)/shard_map/ppermute | solution.py:20
  224.8 5.5 %fusion.1 = (f32[]{:T(128)}, f32[]{:T(128)}) fusion(bf16[1,512,4096]{2,1,0:T(8,128)(2,1)} %param.13, bf16[1,512,4096]{2,1,0:T(8,128)(2,1)S(1)} %copy-done.1), kind=kLoop, calls=%fused_computation.3 | loop fusion | flops 12582910 | bytes 8388616 | tf_op jit(solution)/shard_map/reduce_sum | solution.py:200
  233.0 2.1 collective-permute-start.22
  237.8 2.6 collective-permute-done.22
  241.7 3.2 stack.32
  244.9 2.8 collective-permute-start.25
  253.0 2.5 collective-permute-start.29
  259.5 2.8 collective-permute-start.32
  275.0 2.2 copy-done.2
  277.2 14.7 %finish.1 = (f32[512,4096]{1,0:T(8,128)}, f32[16,8,256]{2,1,0:T(8,128)S(1)}) custom-call(f32[2]{0:T(128)S(1)} %pad_maximum_fusion.coef_ref, bf16[512,768]{1,0:T(8,128)(2,1)S(1)} %bitcast.170, bf16[16,768,256]{2,1,0:T(8,128)(2,1)} %bitcast.173, bf16[512,4096]{1,0:T(8,128)(2,1)S(1)} %bitcast.167, bf16[512,4096]{1,0:T(8,128)(2,1)} %bitcast.172), custom_call_target="tpu_custom_call" | custom-call | flops 3221225472 | bytes 20971520 | tf_op jit(solution)/shard_map/finish/pallas_call | solution.py:141
  293.8 2.6 collective-permute-start.35
  300.7 3.4 %collective-permute-start.37 = (f32[1]{0:T(128)}, f32[1]{0:T(128)}, u32[]{:S(2)}, u32[]{:S(2)}) collective-permute-start(f32[1]{0:T(128)} %add.448), channel_id=1, source_target_pairs={{0,4},{4,8},{8,12},{12,0},{1,5},{5,9},{9,13},{13,1},{2,6},{6,10},{... | collective-permute-start | bytes 20 | tf_op jit(solution)/shard_map/ppermute | solution.py:20
  304.1 3.7 %collective-permute-start.38 = (f32[1]{0:T(128)}, f32[1]{0:T(128)}, u32[]{:S(2)}, u32[]{:S(2)}) collective-permute-start(f32[1]{0:T(128)} %add.448), channel_id=1, source_target_pairs={{0,8},{4,12},{8,0},{12,4},{1,9},{5,13},{9,1},{13,5},{2,10},{6,14},... | collective-permute-start | bytes 20 | tf_op jit(solution)/shard_map/ppermute | solution.py:20
  315.4 4.5 %collective-permute-start.42 = (f32[1]{0:T(128)}, f32[1]{0:T(128)}, u32[]{:S(2)}, u32[]{:S(2)}) collective-permute-start(f32[1]{0:T(128)} %add.452), channel_id=1, source_target_pairs={{0,64},{32,96},{64,0},{96,32},{1,65},{33,97},{65,1},{97,33},{2,66}... | collective-permute-start | bytes 20 | tf_op jit(solution)/shard_map/ppermute | solution.py:20
  319.9 2.2 collective-permute-start.43
  (166 shorter events, 65.1 us)
Async XLA Ops:
  7.2 111.9 %reduce-scatter.2.cloned.1.call-start = ((), (), s32[]{:S(2)}) async-start(), calls=%async_computation.1 | async-start | bytes 13369344 | tf_op jit(solution)/shard_map/reduce_scatter | solution.py:185
  21.5 253.6 %all-gather.4.cloned.1.call-start = ((), (), s32[]{:S(2)}) async-start(), calls=%async_computation.2 | async-start | bytes 6684672 | tf_op jit(solution)/shard_map/all_gather | solution.py:207
  122.1 8.2 %collective-permute-start.1 = (f32[2,96,256]{2,1,0:T(8,128)S(1)}, f32[2,96,256]{2,1,0:T(8,128)S(1)}, u32[]{:S(2)}, u32[]{:S(2)}) collective-permute-start(f32[2,96,256]{2,1,0:T(8,128)S(1)} %get-tuple-element.19), channel_id=1, source_target_pairs={{0,32},{32,64},{64,96},{96,0},{1,33},{33,65},{65,97},{97,1},{2,34}... | collective-permute-start | bytes 589832 | tf_op jit(solution)/shard_map/ppermute | solution.py:20
  123.9 11.8 %collective-permute-start.2 = (f32[2,96,256]{2,1,0:T(8,128)S(1)}, f32[2,96,256]{2,1,0:T(8,128)S(1)}, u32[]{:S(2)}, u32[]{:S(2)}) collective-permute-start(f32[2,96,256]{2,1,0:T(8,128)S(1)} %get-tuple-element.18), channel_id=1, source_target_pairs={{0,64},{32,96},{64,0},{96,32},{1,65},{33,97},{65,1},{97,33},{2,66}... | collective-permute-start | bytes 589832 | tf_op jit(solution)/shard_map/ppermute | solution.py:20
  126.9 8.8 %collective-permute-start.3 = (f32[2,96,256]{2,1,0:T(8,128)S(1)}, f32[2,96,256]{2,1,0:T(8,128)S(1)}, u32[]{:S(2)}, u32[]{:S(2)}) collective-permute-start(f32[2,96,256]{2,1,0:T(8,128)S(1)} %get-tuple-element.17), channel_id=1, source_target_pairs={{0,96},{32,0},{64,32},{96,64},{1,97},{33,1},{65,33},{97,65},{2,98}... | collective-permute-start | bytes 589832 | tf_op jit(solution)/shard_map/ppermute | solution.py:20
  139.6 6.4 %collective-permute-start.17 = (bf16[2,96,256]{2,1,0:T(8,128)(2,1)S(1)}, bf16[2,96,256]{2,1,0:T(8,128)(2,1)S(1)}, u32[]{:S(2)}, u32[]{:S(2)}) collective-permute-start(bf16[2,96,256]{2,1,0:T(8,128)(2,1)S(1)} %get-tuple-element.25), channel_id=1, source_target_pairs={{0,32},{32,64},{64,96},{96,0},{1,33},{33,65},{65,97},{97,1},{2,34}... | collective-permute-start | bytes 294920 | tf_op jit(solution)/shard_map/ppermute | solution.py:20
  141.1 7.3 %collective-permute-start.18 = (bf16[2,96,256]{2,1,0:T(8,128)(2,1)S(1)}, bf16[2,96,256]{2,1,0:T(8,128)(2,1)S(1)}, u32[]{:S(2)}, u32[]{:S(2)}) collective-permute-start(bf16[2,96,256]{2,1,0:T(8,128)(2,1)S(1)} %get-tuple-element.24), channel_id=1, source_target_pairs={{0,64},{32,96},{64,0},{96,32},{1,65},{33,97},{65,1},{97,33},{2,66}... | collective-permute-start | bytes 294920 | tf_op jit(solution)/shard_map/ppermute | solution.py:20
  143.5 5.0 %collective-permute-start.19 = (bf16[2,96,256]{2,1,0:T(8,128)(2,1)S(1)}, bf16[2,96,256]{2,1,0:T(8,128)(2,1)S(1)}, u32[]{:S(2)}, u32[]{:S(2)}) collective-permute-start(bf16[2,96,256]{2,1,0:T(8,128)(2,1)S(1)} %get-tuple-element.23), channel_id=1, source_target_pairs={{0,96},{32,0},{64,32},{96,64},{1,97},{33,1},{65,33},{97,65},{2,98}... | collective-permute-start | bytes 294920 | tf_op jit(solution)/shard_map/ppermute | solution.py:20
  151.0 11.3 %collective-permute-start.4 = (bf16[192,768]{1,0:T(8,128)(2,1)}, bf16[192,768]{1,0:T(8,128)(2,1)}, u32[]{:S(2)}, u32[]{:S(2)}) collective-permute-start(bf16[192,768]{1,0:T(8,128)(2,1)} %get-tuple-element.12), channel_id=1, source_target_pairs={{0,4},{4,8},{8,12},{12,0},{1,5},{5,9},{9,13},{13,1},{2,6},{6,10},{... | collective-permute-start | bytes 884744 | tf_op jit(solution)/shard_map/ppermute | solution.py:20
  152.1 20.4 %collective-permute-start.5 = (bf16[192,768]{1,0:T(8,128)(2,1)}, bf16[192,768]{1,0:T(8,128)(2,1)}, u32[]{:S(2)}, u32[]{:S(2)}) collective-permute-start(bf16[192,768]{1,0:T(8,128)(2,1)} %get-tuple-element.14), channel_id=1, source_target_pairs={{0,8},{4,12},{8,0},{12,4},{1,9},{5,13},{9,1},{13,5},{2,10},{6,14},... | collective-permute-start | bytes 884744 | tf_op jit(solution)/shard_map/ppermute | solution.py:20
  154.4 19.4 %collective-permute-start.6 = (bf16[192,768]{1,0:T(8,128)(2,1)S(1)}, bf16[192,768]{1,0:T(8,128)(2,1)}, u32[]{:S(2)}, u32[]{:S(2)}) collective-permute-start(bf16[192,768]{1,0:T(8,128)(2,1)S(1)} %get-tuple-element.13), channel_id=1, source_target_pairs={{0,12},{4,0},{8,4},{12,8},{1,13},{5,1},{9,5},{13,9},{2,14},{6,2},{... | collective-permute-start | bytes 884744 | tf_op jit(solution)/shard_map/ppermute | solution.py:20
  175.1 5.6 %collective-permute-start.7 = (bf16[48,768]{1,0:T(8,128)(2,1)S(1)}, bf16[48,768]{1,0:T(8,128)(2,1)S(1)}, u32[]{:S(2)}, u32[]{:S(2)}) collective-permute-start(bf16[48,768]{1,0:T(8,128)(2,1)S(1)} %get-tuple-element.26), channel_id=1, source_target_pairs={{0,1},{1,2},{2,3},{3,0},{4,5},{5,6},{6,7},{7,4},{8,9},{9,10},{10,1... | collective-permute-start | bytes 221192 | tf_op jit(solution)/shard_map/ppermute | solution.py:20
  176.2 5.9 %collective-permute-start.8 = (bf16[48,768]{1,0:T(8,128)(2,1)S(1)}, bf16[48,768]{1,0:T(8,128)(2,1)S(1)}, u32[]{:S(2)}, u32[]{:S(2)}) collective-permute-start(bf16[48,768]{1,0:T(8,128)(2,1)S(1)} %get-tuple-element.28), channel_id=1, source_target_pairs={{0,2},{1,3},{2,0},{3,1},{4,6},{5,7},{6,4},{7,5},{8,10},{9,11},{10,... | collective-permute-start | bytes 221192 | tf_op jit(solution)/shard_map/ppermute | solution.py:20
  182.5 7.0 %collective-permute-start.10 = (bf16[48,768]{1,0:T(8,128)(2,1)S(1)}, bf16[48,768]{1,0:T(8,128)(2,1)S(1)}, u32[]{:S(2)}, u32[]{:S(2)}) collective-permute-start(bf16[48,768]{1,0:T(8,128)(2,1)S(1)} %get-tuple-element.11), channel_id=1, source_target_pairs={{0,1},{1,2},{2,3},{3,0},{4,5},{5,6},{6,7},{7,4},{8,9},{9,10},{10,1... | collective-permute-start | bytes 221192 | tf_op jit(solution)/shard_map/ppermute | solution.py:20
  183.8 9.3 %collective-permute-start.11 = (bf16[48,768]{1,0:T(8,128)(2,1)S(1)}, bf16[48,768]{1,0:T(8,128)(2,1)S(1)}, u32[]{:S(2)}, u32[]{:S(2)}) collective-permute-start(bf16[48,768]{1,0:T(8,128)(2,1)S(1)} %get-tuple-element.11), channel_id=1, source_target_pairs={{0,2},{1,3},{2,0},{3,1},{4,6},{5,7},{6,4},{7,5},{8,10},{9,11},{10,... | collective-permute-start | bytes 221192 | tf_op jit(solution)/shard_map/ppermute | solution.py:20
  186.8 6.3 %collective-permute-start.12 = (bf16[48,768]{1,0:T(8,128)(2,1)S(1)}, bf16[48,768]{1,0:T(8,128)(2,1)S(1)}, u32[]{:S(2)}, u32[]{:S(2)}) collective-permute-start(bf16[48,768]{1,0:T(8,128)(2,1)S(1)} %get-tuple-element.11), channel_id=1, source_target_pairs={{0,3},{1,0},{2,1},{3,2},{4,7},{5,4},{6,5},{7,6},{8,11},{9,8},{10,9... | collective-permute-start | bytes 221192 | tf_op jit(solution)/shard_map/ppermute | solution.py:20
  193.2 17.1 %collective-permute-start.13 = (bf16[192,768]{1,0:T(8,128)(2,1)S(1)}, bf16[192,768]{1,0:T(8,128)(2,1)S(1)}, u32[]{:S(2)}, u32[]{:S(2)}) collective-permute-start(bf16[192,768]{1,0:T(8,128)(2,1)S(1)} %bitcast.181), channel_id=1, source_target_pairs={{0,4},{4,8},{8,12},{12,0},{1,5},{5,9},{9,13},{13,1},{2,6},{6,10},{... | collective-permute-start | bytes 884744 | tf_op jit(solution)/shard_map/ppermute | solution.py:20
  194.5 28.9 %collective-permute-start.14 = (bf16[192,768]{1,0:T(8,128)(2,1)S(1)}, bf16[192,768]{1,0:T(8,128)(2,1)S(1)}, u32[]{:S(2)}, u32[]{:S(2)}) collective-permute-start(bf16[192,768]{1,0:T(8,128)(2,1)S(1)} %bitcast.182), channel_id=1, source_target_pairs={{0,8},{4,12},{8,0},{12,4},{1,9},{5,13},{9,1},{13,5},{2,10},{6,14},... | collective-permute-start | bytes 884744 | tf_op jit(solution)/shard_map/ppermute | solution.py:20
  197.8 25.7 %collective-permute-start.15 = (bf16[192,768]{1,0:T(8,128)(2,1)S(1)}, bf16[192,768]{1,0:T(8,128)(2,1)S(1)}, u32[]{:S(2)}, u32[]{:S(2)}) collective-permute-start(bf16[192,768]{1,0:T(8,128)(2,1)S(1)} %bitcast.183), channel_id=1, source_target_pairs={{0,12},{4,0},{8,4},{12,8},{1,13},{5,1},{9,5},{13,9},{2,14},{6,2},{... | collective-permute-start | bytes 884744 | tf_op jit(solution)/shard_map/ppermute | solution.py:20
  224.7 6.6 %collective-permute-start.20 = (bf16[4,96,256]{2,1,0:T(8,128)(2,1)S(1)}, bf16[4,96,256]{2,1,0:T(8,128)(2,1)S(1)}, u32[]{:S(2)}, u32[]{:S(2)}) collective-permute-start(bf16[4,96,256]{2,1,0:T(8,128)(2,1)S(1)} %dynamic-slice_bitcast_fusion.4), channel_id=1, source_target_pairs={{0,16},{16,0},{1,17},{17,1},{2,18},{18,2},{3,19},{19,3},{4,20},{20... | collective-permute-start | bytes 589832 | tf_op jit(solution)/shard_map/ppermute | solution.py:20
  231.3 6.5 %collective-permute-start.21 = (bf16[2,96,256]{2,1,0:T(8,128)(2,1)S(1)}, bf16[2,96,256]{2,1,0:T(8,128)(2,1)S(1)}, u32[]{:S(2)}, u32[]{:S(2)}) collective-permute-start(bf16[2,96,256]{2,1,0:T(8,128)(2,1)S(1)} %get-tuple-element.22), channel_id=1, source_target_pairs={{0,32},{32,64},{64,96},{96,0},{1,33},{33,65},{65,97},{97,1},{2,34}... | collective-permute-start | bytes 294920 | tf_op jit(solution)/shard_map/ppermute | solution.py:20
  233.0 7.4 %collective-permute-start.22 = (bf16[2,96,256]{2,1,0:T(8,128)(2,1)S(1)}, bf16[2,96,256]{2,1,0:T(8,128)(2,1)S(1)}, u32[]{:S(2)}, u32[]{:S(2)}) collective-permute-start(bf16[2,96,256]{2,1,0:T(8,128)(2,1)S(1)} %get-tuple-element.21), channel_id=1, source_target_pairs={{0,64},{32,96},{64,0},{96,32},{1,65},{33,97},{65,1},{97,33},{2,66}... | collective-permute-start | bytes 294920 | tf_op jit(solution)/shard_map/ppermute | solution.py:20
  235.1 5.4 %collective-permute-start.23 = (bf16[2,96,256]{2,1,0:T(8,128)(2,1)S(1)}, bf16[2,96,256]{2,1,0:T(8,128)(2,1)S(1)}, u32[]{:S(2)}, u32[]{:S(2)}) collective-permute-start(bf16[2,96,256]{2,1,0:T(8,128)(2,1)S(1)} %get-tuple-element.20), channel_id=1, source_target_pairs={{0,96},{32,0},{64,32},{96,64},{1,97},{33,1},{65,33},{97,65},{2,98}... | collective-permute-start | bytes 294920 | tf_op jit(solution)/shard_map/ppermute | solution.py:20
  244.9 5.2 %collective-permute-start.25 = (f32[5]{0:T(128)S(1)}, f32[5]{0:T(128)S(1)}, u32[]{:S(2)}, u32[]{:S(2)}) collective-permute-start(f32[5]{0:T(128)S(1)} %stack.32), channel_id=1, source_target_pairs={{0,2},{1,3},{2,0},{3,1},{4,6},{5,7},{6,4},{7,5},{8,10},{9,11},{10,... | collective-permute-start | bytes 68 | tf_op jit(solution)/shard_map/ppermute | solution.py:20
  251.4 5.2 %collective-permute-start.28 = (f32[5]{0:T(128)S(1)}, f32[5]{0:T(128)S(1)}, u32[]{:S(2)}, u32[]{:S(2)}) collective-permute-start(f32[5]{0:T(128)S(1)} %add_add_fusion.3), channel_id=1, source_target_pairs={{0,8},{4,12},{8,0},{12,4},{1,9},{5,13},{9,1},{13,5},{2,10},{6,14},... | collective-permute-start | bytes 68 | tf_op jit(solution)/shard_map/ppermute | solution.py:20
  259.5 5.1 %collective-permute-start.32 = (f32[5]{0:T(128)S(1)}, f32[5]{0:T(128)S(1)}, u32[]{:S(2)}, u32[]{:S(2)}) collective-permute-start(f32[5]{0:T(128)S(1)} %add.437), channel_id=1, source_target_pairs={{0,64},{32,96},{64,0},{96,32},{1,65},{33,97},{65,1},{97,33},{2,66}... | collective-permute-start | bytes 68 | tf_op jit(solution)/shard_map/ppermute | solution.py:20
  292.6 5.0 %collective-permute-start.34 = (f32[1]{0:T(128)}, f32[1]{0:T(128)}, u32[]{:S(2)}, u32[]{:S(2)}) collective-permute-start(f32[1]{0:T(128)} %bitcast.84), channel_id=1, source_target_pairs={{0,1},{1,2},{2,3},{3,0},{4,5},{5,6},{6,7},{7,4},{8,9},{9,10},{10,1... | collective-permute-start | bytes 20 | tf_op jit(solution)/shard_map/ppermute | solution.py:20
  293.8 5.2 %collective-permute-start.35 = (f32[1]{0:T(128)}, f32[1]{0:T(128)}, u32[]{:S(2)}, u32[]{:S(2)}) collective-permute-start(f32[1]{0:T(128)} %bitcast.84), channel_id=1, source_target_pairs={{0,2},{1,3},{2,0},{3,1},{4,6},{5,7},{6,4},{7,5},{8,10},{9,11},{10,... | collective-permute-start | bytes 20 | tf_op jit(solution)/shard_map/ppermute | solution.py:20
  300.7 8.7 %collective-permute-start.37 = (f32[1]{0:T(128)}, f32[1]{0:T(128)}, u32[]{:S(2)}, u32[]{:S(2)}) collective-permute-start(f32[1]{0:T(128)} %add.448), channel_id=1, source_target_pairs={{0,4},{4,8},{8,12},{12,0},{1,5},{5,9},{9,13},{13,1},{2,6},{6,10},{... | collective-permute-start | bytes 20 | tf_op jit(solution)/shard_map/ppermute | solution.py:20
  304.1 5.8 %collective-permute-start.38 = (f32[1]{0:T(128)}, f32[1]{0:T(128)}, u32[]{:S(2)}, u32[]{:S(2)}) collective-permute-start(f32[1]{0:T(128)} %add.448), channel_id=1, source_target_pairs={{0,8},{4,12},{8,0},{12,4},{1,9},{5,13},{9,1},{13,5},{2,10},{6,14},... | collective-permute-start | bytes 20 | tf_op jit(solution)/shard_map/ppermute | solution.py:20
  314.0 8.1 %collective-permute-start.41 = (f32[1]{0:T(128)}, f32[1]{0:T(128)}, u32[]{:S(2)}, u32[]{:S(2)}) collective-permute-start(f32[1]{0:T(128)} %add.452), channel_id=1, source_target_pairs={{0,32},{32,64},{64,96},{96,0},{1,33},{33,65},{65,97},{97,1},{2,34}... | collective-permute-start | bytes 20 | tf_op jit(solution)/shard_map/ppermute | solution.py:20
  315.4 7.3 %collective-permute-start.42 = (f32[1]{0:T(128)}, f32[1]{0:T(128)}, u32[]{:S(2)}, u32[]{:S(2)}) collective-permute-start(f32[1]{0:T(128)} %add.452), channel_id=1, source_target_pairs={{0,64},{32,96},{64,0},{96,32},{1,65},{33,97},{65,1},{97,33},{2,66}... | collective-permute-start | bytes 20 | tf_op jit(solution)/shard_map/ppermute | solution.py:20
  (25 other events, 106.7 us)
Sparse Core Ops, SparseCore 0:
  21.6 97.4 reduce-scatter.1
  149.4 75.5 all-gather.3

commit v2 on v1

v2 whole, which is shorter than its diff:
```python
import math

import jax
import jax.numpy as jnp
from jax import lax
from jax.experimental import pallas as pl
from jax.experimental.pallas import tpu as pltpu
from jax.sharding import Mesh
from jax.sharding import PartitionSpec as P

EXPERT_FSDP = ("expert_0", "expert_1", "fsdp_0", "fsdp_1")
EXPERT = ("expert_0", "expert_1")
FSDP = ("fsdp_0", "fsdp_1")
PARAMS = dict(vmem_limit_bytes=60 * 1024 * 1024)
CHUNKS = 1
SPAN = 512


def shift(array, axis, amount):
    size = lax.axis_size(axis)
    return lax.ppermute(array, axis, [(i, (i + amount) % size) for i in range(size)])


def pick(array, index):
    return lax.dynamic_index_in_dim(array, index, 0, keepdims=False)


def exchange_axis(blocks, axis):
    size = lax.axis_size(axis)
    me = lax.axis_index(axis)
    received = [(me, pick(blocks, me))]
    for step in range(1, size):
        sent = pick(blocks, (me + step) % size)
        received.append(((me - step) % size, shift(sent, axis, step)))
    return received


def gather_axis(block, axis):
    size = lax.axis_size(axis)
    me = lax.axis_index(axis)
    array = jnp.zeros((size,) + block.shape, block.dtype)
    array = lax.dynamic_update_index_in_dim(array, block, me, 0)
    for step in range(1, size):
        arrived = shift(block, axis, step)
        array = lax.dynamic_update_index_in_dim(array, arrived, (me - step) % size, 0)
    return array


def relative(rows):
    outer, inner = lax.axis_size("expert_0"), lax.axis_size("expert_1")
    chip, core = lax.axis_index("expert_0"), lax.axis_index("expert_1")
    blocks = rows.reshape((outer, inner, -1) + rows.shape[1:])
    blocks = jnp.where(core == 0, blocks, blocks[:, ::-1])
    twice = jnp.concatenate([blocks, blocks], axis=0)
    return lax.dynamic_slice_in_dim(twice, chip, outer, 0).reshape(rows.shape)


def expert_exchange(rows, sign):
    outer, inner = lax.axis_size("expert_0"), lax.axis_size("expert_1")
    block = rows.shape[0] // (outer * inner)
    blocks = rows.reshape((outer, inner, block) + rows.shape[1:])
    other = shift(blocks[:, 1], "expert_1", 1)
    out = []
    for step in range(outer):
        pair = jnp.stack([blocks[step, 0], other[step]])
        out.append(shift(pair, "expert_0", sign * step) if step else pair)
    return jnp.concatenate(out).reshape(rows.shape)


def gram(hidden):
    partial = lax.dot_general(
        hidden, hidden, (((1,), (1,)), ((), ())), preferred_element_type=jnp.float32
    )
    size = partial.shape[0]
    block = partial
    for axis in FSDP:
        parts = lax.axis_size(axis)
        block = block.reshape(parts, -1, size).astype(jnp.bfloat16)
        terms = exchange_axis(block, axis)
        block = sum(term.astype(jnp.float32) for _, term in terms)
    block = block.astype(jnp.bfloat16)
    for axis in FSDP[::-1]:
        block = gather_axis(block, axis).reshape(-1, size)
    return block


def all_sum(values):
    for axis in EXPERT_FSDP[::-1]:
        size = lax.axis_size(axis)
        values = sum([values] + [shift(values, axis, step) for step in range(1, size)])
    return values


def gate_tables(packed, experts, capacity):
    blocks, tokens, _ = packed.shape
    top = (packed.shape[2] - 1) // 2
    outer, inner = lax.axis_size("expert_0"), lax.axis_size("expert_1")
    chip, core = lax.axis_index("expert_0"), lax.axis_index("expert_1")
    ids = packed[:, :, :top].reshape(blocks, tokens * top).astype(jnp.int32)
    gates = packed[:, :, top : 2 * top].reshape(blocks, tokens * top)
    same = ids[:, :, None] == ids[:, None, :]
    order = jnp.arange(tokens * top)
    earlier = order[None, :] < order[:, None]
    slots = jnp.sum((same & earlier[None]).astype(jnp.int32), axis=2)
    places = (chip - ids // inner) % outer * inner + (core - ids % inner) % inner
    column = places * (blocks * capacity) + jnp.arange(blocks)[:, None] * capacity + slots
    columns = jnp.arange(experts * blocks * capacity)
    hits = column[:, :, None] == columns[None, None, :]
    weighted = jnp.where(hits, gates[:, :, None], 0.0)
    weighted = weighted.reshape(blocks * tokens, top, -1)
    return jnp.sum(weighted, axis=1), packed[:, :, 2 * top].reshape(-1)


def outputs_kernel(hidden_ref, side_ref, out_ref):
    group, rows, width = out_ref.shape
    tile = rows // 3

    @pl.loop(0, 3)
    def _(i):
        part = pl.ds(pl.multiple_of(i * tile, tile), tile)
        product = jnp.dot(hidden_ref[part, :], side_ref[...], preferred_element_type=jnp.float32)
        for k in range(group):
            out_ref[k, part, :] = product[:, k * width : (k + 1) * width]


def expert_outputs(hidden, side, parts, chunk):
    rows, depth = hidden.shape
    width = side.shape[1] // parts // CHUNKS
    group = SPAN // width
    steps = parts // group
    return pl.pallas_call(
        outputs_kernel,
        grid=(steps,),
        in_specs=[
            pl.BlockSpec((rows, depth), lambda i: (0, 0)),
            pl.BlockSpec((depth, group * width), lambda i: (0, chunk * steps + i)),
        ],
        out_specs=pl.BlockSpec((group, rows, width), lambda i: (i, 0, 0)),
        out_shape=jax.ShapeDtypeStruct((parts, rows, width), jnp.float32),
        compiler_params=pltpu.CompilerParams(**PARAMS),
        cost_estimate=pl.CostEstimate(
            flops=2 * rows * depth * parts * width,
            bytes_accessed=4 * rows * parts * width,
            transcendentals=0,
        ),
        name="expert_outputs",
    )(hidden, side)


def finish_kernel(coef_ref, hidden_ref, tangent_ref, side_ref, held_ref, out_ref):
    group = tangent_ref.shape[0]
    tangents = jnp.concatenate([tangent_ref[k] for k in range(group)], axis=1)
    image = jnp.dot(hidden_ref[...], tangents, preferred_element_type=jnp.float32)
    out_ref[...] = coef_ref[0] * side_ref[...].astype(jnp.float32) + coef_ref[1] * image


def finish(coefs, hidden_t, tangents, side, held, chunk):
    parts, rows, width = tangents.shape
    depth = hidden_t.shape[0]
    group = SPAN // width
    steps = parts // group
    column = pl.BlockSpec((depth, group * width), lambda i: (0, chunk * steps + i))
    specs = [
        pl.BlockSpec(memory_space=pltpu.SMEM),
        pl.BlockSpec((depth, rows), lambda i: (0, 0)),
        pl.BlockSpec((group, rows, width), lambda i: (i, 0, 0)),
        column,
    ]
    args = [coefs, hidden_t, tangents, side]
    kernel = lambda c, h, t, s, o: finish_kernel(c, h, t, s, None, o)
    aliases = {}
    if held is not None:
        kernel = finish_kernel
        specs.append(pl.BlockSpec(memory_space=pl.ANY))
        args.append(held)
        aliases = {4: 0}
    return pl.pallas_call(
        kernel,
        grid=(steps,),
        in_specs=specs,
        out_specs=column,
        out_shape=jax.ShapeDtypeStruct(side.shape, jnp.float32),
        input_output_aliases=aliases,
        compiler_params=pltpu.CompilerParams(**PARAMS),
        cost_estimate=pl.CostEstimate(
            flops=2 * rows * depth * parts * width,
            bytes_accessed=8 * depth * parts * width,
            transcendentals=0,
        ),
        name="finish",
    )(*args)


def mix(table, rows):
    return jnp.dot(
        table, rows, precision=lax.Precision.HIGHEST, preferred_element_type=jnp.float32
    )


def local(hidden, expert_ids, gate_weights, loss_weight, decay, val_grad, down_weight):
    n_expert = lax.axis_size(EXPERT)
    n_fsdp = lax.axis_size(FSDP)
    capacity = hidden.shape[1] // (n_expert * n_fsdp)
    tokens, top = expert_ids.shape
    rate = decay[0]
    side, target = val_grad[0], down_weight[0]
    acts = relative(hidden[0])
    rows = acts.shape[0]

    summed = []
    for chunk in range(CHUNKS):
        partial = expert_outputs(acts, side, n_fsdp, chunk)
        summed.append(
            lax.psum_scatter(
                partial.reshape(n_fsdp * rows, -1), FSDP, scatter_dimension=0, tiled=True
            )
        )

    packed = jnp.concatenate(
        [expert_ids.astype(jnp.float32), gate_weights, loss_weight[:, None]], axis=1
    )
    share = n_fsdp // n_expert
    for axis in EXPERT_FSDP[::-1]:
        packed = gather_axis(packed, axis)
    everyone = packed.reshape(n_expert, n_fsdp, tokens, -1)
    mine = lax.dynamic_slice_in_dim(everyone, lax.axis_index(EXPERT) * share, share, 1)
    mine = mine.swapaxes(0, 1).reshape(share * n_expert, tokens, -1)
    table, weights = gate_tables(mine, n_expert, capacity)
    kernel_matrix = gram(acts)
    wide = side.astype(jnp.float32)
    norm = jnp.sum(wide * wide)
    fixed = jnp.sum(target.astype(jnp.float32) * wide)
    targets = [expert_outputs(acts, target, n_fsdp, chunk) for chunk in range(CHUNKS)]
    acts_t = acts.T
    summed[0], table, weights, kernel_matrix, norm, fixed, targets, acts_t = (
        lax.optimization_barrier(
            (summed[0], table, weights, kernel_matrix, norm, fixed, targets, acts_t)
        )
    )

    returned, tangents = [], []
    bg = gg = ghg = wg = 0.0
    for chunk in range(CHUNKS):
        mixed = mix(table, expert_exchange(summed[chunk], 1))
        scaled = weights[:, None] * mixed
        bg += jnp.sum(scaled * mixed)
        leaving = mix(table.T, scaled).astype(jnp.bfloat16)
        returned.append(expert_exchange(leaving, -1))
        gathered = lax.all_gather(returned[chunk], FSDP, axis=0, tiled=True)
        tangents.append(gathered.reshape(n_fsdp, rows, -1))
    for chunk in range(CHUNKS):
        second = jnp.dot(kernel_matrix, returned[chunk], preferred_element_type=jnp.float32)
        gg += jnp.sum(second * returned[chunk].astype(jnp.float32))
        exchanged = expert_exchange(second.astype(jnp.bfloat16), 1)
        again = mix(table, exchanged.astype(jnp.float32))
        ghg += jnp.sum(weights[:, None] * again * again)
    bb, bg, gg, ghg, wb = all_sum(jnp.stack([norm, bg, gg, ghg, fixed]))
    alpha = bb / (bg + rate * bb)
    lean = bg / bb
    across = gg - bg * lean
    fresh = alpha * alpha * across
    beta = fresh / bb
    bent = ghg - 2.0 * lean * gg + lean * lean * bg
    curve = alpha * alpha * (bent + rate * across) - beta * fresh / alpha
    step = fresh / curve
    keep = alpha + step * (beta + alpha * lean)
    move = -step * alpha

    for chunk in range(CHUNKS):
        wg += jnp.sum(targets[chunk] * tangents[chunk].astype(jnp.float32))
    wg = all_sum(jnp.reshape(wg, (1,)))[0]
    result = None
    for chunk in range(CHUNKS):
        result = finish(jnp.stack([keep, move]), acts_t, tangents[chunk], side, result, chunk)
    hyper = -(keep * wb + move * wg) / math.sqrt(n_expert * side.shape[1])
    return (result[None], jnp.reshape(hyper, (1,)))


def solution(mesh):
    finer = Mesh(mesh.devices.reshape(4, 2, 4, 4), EXPERT_FSDP)
    specs = (
        P(EXPERT, None, FSDP),
        P(EXPERT_FSDP, None),
        P(EXPERT_FSDP, None),
        P(EXPERT_FSDP),
        P(),
        P(EXPERT, FSDP, None),
        P(EXPERT, FSDP, None),
    )
    return jax.shard_map(
        local, mesh=finer, in_specs=specs, out_specs=(P(EXPERT, FSDP, None), P()), check_vma=False
    )
```

time: 333 us -> 295 us (0.89)
  blocking collectives: 61.3 us -> 0 us
  starting transfers between devices: 69.9 us -> 84.6 us
  waiting for transfers between devices: 116 us -> 102 us
  other arithmetic: 8.27 us -> 21.6 us
  Pallas kernels: 25.6 us -> 35.1 us
  local copies, waits for them, and re-layouts: 14.7 us -> 11.3 us
    all_gather x1 -> x0, blocking collectives: 61.3 us -> none  [local(): lax.all_gather(packed, EXPERT_FSDP).reshape(n_expert, n_fsdp, tokens, -1)]
    ppermute x44 -> x54, starting transfers between devices: 69.8 us -> 84.5 us  [shift(): lax.ppermute(array, axis, [(i, (i + amount) % size) for i in range(size)])]
    reduce_scatter x1, waiting for transfers between devices: 34.9 us -> 21.8 us  [local(): lax.psum_scatter(partial.reshape(n_fsdp * rows, -1), FSDP, scatter_dimens...]
    reduce_sum x1, other arithmetic: 0.63 us -> 10.3 us  [local(): wg += jnp.sum(targets[chunk] * tangents[chunk].astype(jnp.float32))]
    pallas_call x2 -> x3, Pallas kernels: 25.6 us -> 35.1 us  [the longest x2 23.5 us: expert_outputs(): pl.pallas_call(outputs_kernel, grid=(steps,), in_specs=[pl.BlockSpec((row...]
    all_gather x1, waiting for transfers between devices: 0.01 us -> 9.14 us  [local(): gathered = lax.all_gather(returned[chunk], FSDP, axis=0, tiled=True)]
    ppermute x44 -> x54, waiting for transfers between devices: 80.6 us -> 71.5 us  [shift(): lax.ppermute(array, axis, [(i, (i + amount) % size) for i in range(size)])]
    unnamed x23 -> x19, local copies, waits for them, and re-layouts: 7.13 us -> 2.32 us
  transfers between devices with their start and end apart: 46 -> 56, of which waited for: 36 -> 34; matrix products, arithmetic and copies ran while one was open for 5% -> 7% of each run, Pallas kernels for 0% -> 8%
where the time goes in v2:
time: 295 us; the launch traced here: 293 us
  waiting for transfers between devices  102 us (35%)
  starting transfers between devices  84.6 us (29%)
  Pallas kernels  35.1 us (12%)
  between operations  32 us (11%)
  other arithmetic  21.6 us (7%)
  local copies, waits for them, and re-layouts  11.3 us (4%)
  matrix products  6.47 us (2%)
    ppermute x54, starting transfers between devices, shift(): lax.ppermute(array, axis, [(i, (i + amount) % size) for i in range(size)])  84.5 us
    ppermute x54, waiting for transfers between devices, shift(): lax.ppermute(array, axis, [(i, (i + amount) % size) for i in range(size)])  71.5 us
    pallas_call x2, Pallas kernels, expert_outputs(): pl.pallas_call(outputs_kernel, grid=(steps,), in_specs=[pl.BlockSpec((row...  23.5 us
    reduce_scatter x1, waiting for transfers between devices, local(): lax.psum_scatter(partial.reshape(n_fsdp * rows, -1), FSDP, scatter_dimens...  21.8 us
    pallas_call x1, Pallas kernels, finish(): pl.pallas_call(kernel, grid=(steps,), in_specs=specs, out_specs=column, o...  11.6 us
    reduce_sum x1, other arithmetic, local(): wg += jnp.sum(targets[chunk] * tangents[chunk].astype(jnp.float32))  10.3 us
    all_gather x1, waiting for transfers between devices, local(): gathered = lax.all_gather(returned[chunk], FSDP, axis=0, tiled=True)  9.14 us
    reduce_sum x1, other arithmetic, local(): fixed = jnp.sum(target.astype(jnp.float32) * wide)  6.66 us
  transfers between devices with their start and end apart: 56, of which 34 were waited for; matrix products, arithmetic and copies ran while one was open for 7% of the time, Pallas kernels for 8%

profile of v2, /device:TPU:0, one launch (start us, length us, event | category | flops | bytes accessed | tf_op | source)
XLA Modules:
  0.0 293.5 jit_solution(10011612451573233523)
XLA Ops:
  10.0 11.7 %expert_outputs.2 = f32[16,768,256]{2,1,0:T(8,128)} custom-call(bf16[768,512]{1,0:T(8,128)(2,1)} %bitcast.185, bf16[512,4096]{1,0:T(8,128)(2,1)} %bitcast.180), custom_call_target="tpu_custom_call" | custom-call | flops 3221225472 | bytes 12582912 | tf_op jit(solution)/shard_map/expert_outputs/pallas_call | solution.py:131
  24.1 2.7 collective-permute-start.1
  30.8 2.9 collective-permute-start.11
  35.0 11.8 %expert_outputs.3 = f32[16,768,256]{2,1,0:T(8,128)} custom-call(bf16[768,512]{1,0:T(8,128)(2,1)} %bitcast.186, bf16[512,4096]{1,0:T(8,128)(2,1)} %bitcast.184), custom_call_target="tpu_custom_call" | custom-call | flops 3221225472 | bytes 12582912 | tf_op jit(solution)/shard_map/expert_outputs/pallas_call | solution.py:131
  46.8 6.7 %fusion.1 = (f32[]{:T(128)}, f32[]{:T(128)}) fusion(bf16[1,512,4096]{2,1,0:T(8,128)(2,1)} %param.13, bf16[1,512,4096]{2,1,0:T(8,128)(2,1)} %param.12), kind=kLoop, calls=%fused_computation.4 | loop fusion | flops 12582910 | bytes 8388616 | tf_op jit(solution)/shard_map/reduce_sum | solution.py:232
  56.7 3.4 %collective-permute-done.3 = f32[4,16,5]{1,0,2:T(4,128)S(1)} collective-permute-done((f32[4,16,5]{1,0,2:T(4,128)S(1)}, f32[4,16,5]{1,0,2:T(4,128)S(1)}, u32[]{:S(2)}, u32[]{:S(2)}) %collective-permute-start.3) | collective-permute-done | bytes 1312 | tf_op jit(solution)/shard_map/ppermute | solution.py:21
  61.4 7.9 %collective-permute-done.5 = f32[4,16,5]{1,0,2:T(4,128)S(1)} collective-permute-done((f32[4,16,5]{1,0,2:T(4,128)S(1)}, f32[4,16,5]{1,0,2:T(4,128)S(1)}, u32[]{:S(2)}, u32[]{:S(2)}) %collective-permute-start.5) | collective-permute-done | bytes 1312 | tf_op jit(solution)/shard_map/ppermute | solution.py:21
  72.4 3.8 %collective-permute-start.8 = (f32[2,4,4,16,5]{3,2,4,1,0:T(4,128)S(1)}, f32[2,4,4,16,5]{3,2,4,1,0:T(4,128)S(1)}, u32[]{:S(2)}, u32[]{:S(2)}) collective-permute-start(f32[2,4,4,16,5]{3,2,4,1,0:T(4,128)S(1)} %bitcast_dynamic-update-slice_fusion.8), channel_id=1, source_target_pairs={{0,64},{32,96},{64,0},{96,32},{1,65},{33,97},{65,1},{97,33},{2,66}... | collective-permute-start | bytes 30728 | tf_op jit(solution)/shard_map/ppermute | solution.py:21
  77.5 2.6 collective-permute-start.9
  86.1 4.8 %collective-permute-done.13 = bf16[48,768]{1,0:T(8,128)(2,1)S(1)} collective-permute-done((bf16[48,768]{1,0:T(8,128)(2,1)S(1)}, bf16[48,768]{1,0:T(8,128)(2,1)S(1)}, u32[]{:S(2)}, u32[]{:S(2)}) %collective-permute-start.13) | collective-permute-done | bytes 73760 | tf_op jit(solution)/shard_map/ppermute | solution.py:21
  97.9 4.0 %collective-permute-done.16 = bf16[48,768]{1,0:T(8,128)(2,1)S(1)} collective-permute-done((bf16[48,768]{1,0:T(8,128)(2,1)S(1)}, bf16[48,768]{1,0:T(8,128)(2,1)S(1)}, u32[]{:S(2)}, u32[]{:S(2)}) %collective-permute-start.16) | collective-permute-done | bytes 73760 | tf_op jit(solution)/shard_map/ppermute | solution.py:21
  105.8 3.1 %collective-permute-start.20 = (bf16[192,768]{1,0:T(8,128)(2,1)S(1)}, bf16[192,768]{1,0:T(8,128)(2,1)S(1)}, u32[]{:S(2)}, u32[]{:S(2)}) collective-permute-start(bf16[192,768]{1,0:T(8,128)(2,1)S(1)} %bitcast.197), channel_id=1, source_target_pairs={{0,8},{4,12},{8,0},{12,4},{1,9},{5,13},{9,1},{13,5},{2,10},{6,14},... | collective-permute-start | bytes 884744 | tf_op jit(solution)/shard_map/ppermute | solution.py:21
  109.7 5.4 %collective-permute-done.19 = bf16[192,768]{1,0:T(8,128)(2,1)S(1)} collective-permute-done((bf16[192,768]{1,0:T(8,128)(2,1)S(1)}, bf16[192,768]{1,0:T(8,128)(2,1)S(1)}, u32[]{:S(2)}, u32[]{:S(2)}) %collective-permute-start.19) | collective-permute-done | bytes 294944 | tf_op jit(solution)/shard_map/ppermute | solution.py:21
  115.1 4.7 %collective-permute-done.20 = bf16[192,768]{1,0:T(8,128)(2,1)S(1)} collective-permute-done((bf16[192,768]{1,0:T(8,128)(2,1)S(1)}, bf16[192,768]{1,0:T(8,128)(2,1)S(1)}, u32[]{:S(2)}, u32[]{:S(2)}) %collective-permute-start.20) | collective-permute-done | bytes 294944 | tf_op jit(solution)/shard_map/ppermute | solution.py:21
  119.9 21.8 %reduce-scatter.2.cloned.1.call-done = f32[768,256]{1,0:T(8,128)} async-done(((f32[12288,256]{1,0:T(8,128)}), f32[768,256]{1,0:T(8,128)}) %reduce-scatter.2.cloned.1.call-update) | async-done | bytes 786448 | tf_op jit(solution)/shard_map/reduce_scatter | solution.py:214
  146.4 3.0 %collective-permute-start.24 = (f32[2,96,256]{2,1,0:T(8,128)S(1)}, f32[2,96,256]{2,1,0:T(8,128)S(1)}, u32[]{:S(2)}, u32[]{:S(2)}) collective-permute-start(f32[2,96,256]{2,1,0:T(8,128)S(1)} %pad_maximum_fusion.1), channel_id=1, source_target_pairs={{0,64},{32,96},{64,0},{96,32},{1,65},{33,97},{65,1},{97,33},{2,66}... | collective-permute-start | bytes 589832 | tf_op jit(solution)/shard_map/ppermute | solution.py:21
  150.8 2.5 collective-permute-done.23
  153.4 5.4 %collective-permute-done.24 = f32[2,96,256]{2,1,0:T(8,128)S(1)} collective-permute-done((f32[2,96,256]{2,1,0:T(8,128)S(1)}, f32[2,96,256]{2,1,0:T(8,128)S(1)}, u32[]{:S(2)}, u32[]{:S(2)}) %collective-permute-start.24) | collective-permute-done | bytes 196640 | tf_op jit(solution)/shard_map/ppermute | solution.py:21
  167.6 2.7 collective-permute-done.27
  181.3 6.0 %collective-permute-done.31 = bf16[2,96,256]{2,1,0:T(8,128)(2,1)S(1)} collective-permute-done((bf16[2,96,256]{2,1,0:T(8,128)(2,1)S(1)}, bf16[2,96,256]{2,1,0:T(8,128)(2,1)S(1)}, u32[]{:S(2)}, u32[]{:S(2)}) %collective-permute-start.31) | collective-permute-done | bytes 98336 | tf_op jit(solution)/shard_map/ppermute | solution.py:21
  188.5 3.2 %stack.68 = f32[5]{0:T(128)S(1)} concatenate(f32[1]{0:T(128)} %bitcast.47, f32[1]{0:T(128)} %bitcast.55, f32[1]{0:T(128)} %bitcast.63, f32[1]{0:T(128)} %bitcast.71, f32[1]{0:T(128)} %bitcast.72), dimensions={0} | concatenate | bytes 40 | tf_op jit(solution)/shard_map/stack | solution.py:257
  192.6 2.4 collective-permute-start.35
  206.2 3.0 %collective-permute-start.42 = (f32[5]{0:T(128)S(1)}, f32[5]{0:T(128)S(1)}, u32[]{:S(2)}, u32[]{:S(2)}) collective-permute-start(f32[5]{0:T(128)S(1)} %add.395), channel_id=1, source_target_pairs={{0,64},{32,96},{64,0},{96,32},{1,65},{33,97},{65,1},{97,33},{2,66}... | collective-permute-start | bytes 68 | tf_op jit(solution)/shard_map/ppermute | solution.py:21
  222.7 9.1 %all-gather.2.cloned.1.call-done = bf16[12288,256]{1,0:T(8,128)(2,1)} async-done(((bf16[768,256]{1,0:T(8,128)(2,1)}), bf16[12288,256]{1,0:T(8,128)(2,1)}) %all-gather.2.cloned.1.call-update) | async-done | bytes 6291472 | tf_op jit(solution)/shard_map/all_gather | solution.py:249
  231.9 10.3 %multiply_reduce_fusion = f32[]{:T(128)} fusion(f32[16,768,256]{2,1,0:T(8,128)} %expert_outputs.3, bf16[16,768,256]{2,1,0:T(8,128)(2,1)} %bitcast.182), kind=kLoop, calls=%fused_computation | loop fusion | flops 9437183 | bytes 18874372 | tf_op jit(solution)/shard_map/reduce_sum | solution.py:270
  243.6 2.7 collective-permute-start.45
  247.8 11.6 %finish.1 = f32[512,4096]{1,0:T(8,128)} custom-call(f32[2]{0:T(128)} %pad_maximum_fusion.10.c, bf16[512,768]{1,0:T(8,128)(2,1)} %bitcast.191, bf16[16,768,256]{2,1,0:T(8,128)(2,1)} %bitcast.183, bf16[512,4096]{1,0:T(8,128)(2,1)} %bitcast.181), custom_call_target="tpu_custom_call" | custom-call | flops 3221225472 | bytes 16777216 | tf_op jit(solution)/shard_map/finish/pallas_call | solution.py:177
  263.6 3.7 %collective-permute-start.48 = (f32[1]{0:T(128)}, f32[1]{0:T(128)}, u32[]{:S(2)}, u32[]{:S(2)}) collective-permute-start(f32[1]{0:T(128)} %add.406), channel_id=1, source_target_pairs={{0,8},{4,12},{8,0},{12,4},{1,9},{5,13},{9,1},{13,5},{2,10},{6,14},... | collective-permute-start | bytes 20 | tf_op jit(solution)/shard_map/ppermute | solution.py:21
  267.3 2.8 collective-permute-start.49
  273.9 2.9 collective-permute-start.51
  276.8 4.2 %collective-permute-start.52 = (f32[1]{0:T(128)}, f32[1]{0:T(128)}, u32[]{:S(2)}, u32[]{:S(2)}) collective-permute-start(f32[1]{0:T(128)} %add.410), channel_id=1, source_target_pairs={{0,64},{32,96},{64,0},{96,32},{1,65},{33,97},{65,1},{97,33},{2,66}... | collective-permute-start | bytes 20 | tf_op jit(solution)/shard_map/ppermute | solution.py:21
  281.0 2.7 collective-permute-start.53
  (196 shorter events, 86.2 us)
Async XLA Ops:
  7.2 134.5 %reduce-scatter.2.cloned.1.call-start = ((), (), s32[]{:S(2)}) async-start(), calls=%async_computation.1 | async-start | bytes 13369344 | tf_op jit(solution)/shard_map/reduce_scatter | solution.py:214
  21.7 210.1 %all-gather.2.cloned.1.call-start = ((), (), s32[]{:S(2)}) async-start(), calls=%async_computation.2 | async-start | bytes 6684672 | tf_op jit(solution)/shard_map/all_gather | solution.py:249
  22.4 31.1 %collective-permute-start = (f32[16,5]{0,1:T(8,128)S(1)}, f32[16,5]{0,1:T(8,128)S(1)}, u32[]{:S(2)}, u32[]{:S(2)}) collective-permute-start(f32[16,5]{0,1:T(8,128)S(1)} %get-tuple-element.55), channel_id=1, source_target_pairs={{0,1},{1,2},{2,3},{3,0},{4,5},{5,6},{6,7},{7,4},{8,9},{9,10},{10,1... | collective-permute-start | bytes 968 | tf_op jit(solution)/shard_map/ppermute | solution.py:21
  24.1 30.9 %collective-permute-start.1 = (f32[16,5]{0,1:T(8,128)S(1)}, f32[16,5]{0,1:T(8,128)S(1)}, u32[]{:S(2)}, u32[]{:S(2)}) collective-permute-start(f32[16,5]{0,1:T(8,128)S(1)} %get-tuple-element.55), channel_id=1, source_target_pairs={{0,2},{1,3},{2,0},{3,1},{4,6},{5,7},{6,4},{7,5},{8,10},{9,11},{10,... | collective-permute-start | bytes 968 | tf_op jit(solution)/shard_map/ppermute | solution.py:21
  26.8 28.2 %collective-permute-start.2 = (f32[16,5]{0,1:T(8,128)S(1)}, f32[16,5]{0,1:T(8,128)S(1)}, u32[]{:S(2)}, u32[]{:S(2)}) collective-permute-start(f32[16,5]{0,1:T(8,128)S(1)} %get-tuple-element.55), channel_id=1, source_target_pairs={{0,3},{1,0},{2,1},{3,2},{4,7},{5,4},{6,5},{7,6},{8,11},{9,8},{10,9... | collective-permute-start | bytes 968 | tf_op jit(solution)/shard_map/ppermute | solution.py:21
  29.1 53.1 %collective-permute-start.10 = (bf16[192,768]{1,0:T(8,128)(2,1)S(1)}, bf16[192,768]{1,0:T(8,128)(2,1)S(1)}, u32[]{:S(2)}, u32[]{:S(2)}) collective-permute-start(bf16[192,768]{1,0:T(8,128)(2,1)S(1)} %get-tuple-element.24), channel_id=1, source_target_pairs={{0,4},{4,8},{8,12},{12,0},{1,5},{5,9},{9,13},{13,1},{2,6},{6,10},{... | collective-permute-start | bytes 884744 | tf_op jit(solution)/shard_map/ppermute | solution.py:21
  30.8 51.4 %collective-permute-start.11 = (bf16[192,768]{1,0:T(8,128)(2,1)S(1)}, bf16[192,768]{1,0:T(8,128)(2,1)S(1)}, u32[]{:S(2)}, u32[]{:S(2)}) collective-permute-start(bf16[192,768]{1,0:T(8,128)(2,1)S(1)} %get-tuple-element.26), channel_id=1, source_target_pairs={{0,8},{4,12},{8,0},{12,4},{1,9},{5,13},{9,1},{13,5},{2,10},{6,14},... | collective-permute-start | bytes 884744 | tf_op jit(solution)/shard_map/ppermute | solution.py:21
  53.5 28.7 %collective-permute-start.12 = (bf16[192,768]{1,0:T(8,128)(2,1)S(1)}, bf16[192,768]{1,0:T(8,128)(2,1)S(1)}, u32[]{:S(2)}, u32[]{:S(2)}) collective-permute-start(bf16[192,768]{1,0:T(8,128)(2,1)S(1)} %get-tuple-element.25), channel_id=1, source_target_pairs={{0,12},{4,0},{8,4},{12,8},{1,13},{5,1},{9,5},{13,9},{2,14},{6,2},{... | collective-permute-start | bytes 884744 | tf_op jit(solution)/shard_map/ppermute | solution.py:21
  60.1 9.1 %collective-permute-start.5 = (f32[4,16,5]{1,0,2:T(4,128)S(1)}, f32[4,16,5]{1,0,2:T(4,128)S(1)}, u32[]{:S(2)}, u32[]{:S(2)}) collective-permute-start(f32[4,16,5]{1,0,2:T(4,128)S(1)} %dynamic_update_slice.75), channel_id=1, source_target_pairs={{0,12},{4,0},{8,4},{12,8},{1,13},{5,1},{9,5},{13,9},{2,14},{6,2},{... | collective-permute-start | bytes 3848 | tf_op jit(solution)/shard_map/ppermute | solution.py:21
  72.4 8.0 %collective-permute-start.8 = (f32[2,4,4,16,5]{3,2,4,1,0:T(4,128)S(1)}, f32[2,4,4,16,5]{3,2,4,1,0:T(4,128)S(1)}, u32[]{:S(2)}, u32[]{:S(2)}) collective-permute-start(f32[2,4,4,16,5]{3,2,4,1,0:T(4,128)S(1)} %bitcast_dynamic-update-slice_fusion.8), channel_id=1, source_target_pairs={{0,64},{32,96},{64,0},{96,32},{1,65},{33,97},{65,1},{97,33},{2,66}... | collective-permute-start | bytes 30728 | tf_op jit(solution)/shard_map/ppermute | solution.py:21
  82.4 8.5 %collective-permute-start.13 = (bf16[48,768]{1,0:T(8,128)(2,1)S(1)}, bf16[48,768]{1,0:T(8,128)(2,1)S(1)}, u32[]{:S(2)}, u32[]{:S(2)}) collective-permute-start(bf16[48,768]{1,0:T(8,128)(2,1)S(1)} %get-tuple-element.42), channel_id=1, source_target_pairs={{0,1},{1,2},{2,3},{3,0},{4,5},{5,6},{6,7},{7,4},{8,9},{9,10},{10,1... | collective-permute-start | bytes 221192 | tf_op jit(solution)/shard_map/ppermute | solution.py:21
  82.9 8.2 %collective-permute-start.14 = (bf16[48,768]{1,0:T(8,128)(2,1)S(1)}, bf16[48,768]{1,0:T(8,128)(2,1)S(1)}, u32[]{:S(2)}, u32[]{:S(2)}) collective-permute-start(bf16[48,768]{1,0:T(8,128)(2,1)S(1)} %get-tuple-element.44), channel_id=1, source_target_pairs={{0,2},{1,3},{2,0},{3,1},{4,6},{5,7},{6,4},{7,5},{8,10},{9,11},{10,... | collective-permute-start | bytes 221192 | tf_op jit(solution)/shard_map/ppermute | solution.py:21
  84.0 9.5 %collective-permute-start.15 = (bf16[48,768]{1,0:T(8,128)(2,1)S(1)}, bf16[48,768]{1,0:T(8,128)(2,1)S(1)}, u32[]{:S(2)}, u32[]{:S(2)}) collective-permute-start(bf16[48,768]{1,0:T(8,128)(2,1)S(1)} %get-tuple-element.43), channel_id=1, source_target_pairs={{0,3},{1,0},{2,1},{3,2},{4,7},{5,4},{6,5},{7,6},{8,11},{9,8},{10,9... | collective-permute-start | bytes 221192 | tf_op jit(solution)/shard_map/ppermute | solution.py:21
  93.6 8.3 %collective-permute-start.16 = (bf16[48,768]{1,0:T(8,128)(2,1)S(1)}, bf16[48,768]{1,0:T(8,128)(2,1)S(1)}, u32[]{:S(2)}, u32[]{:S(2)}) collective-permute-start(bf16[48,768]{1,0:T(8,128)(2,1)S(1)} %get-tuple-element.23), channel_id=1, source_target_pairs={{0,1},{1,2},{2,3},{3,0},{4,5},{5,6},{6,7},{7,4},{8,9},{9,10},{10,1... | collective-permute-start | bytes 221192 | tf_op jit(solution)/shard_map/ppermute | solution.py:21
  94.4 8.2 %collective-permute-start.17 = (bf16[48,768]{1,0:T(8,128)(2,1)S(1)}, bf16[48,768]{1,0:T(8,128)(2,1)S(1)}, u32[]{:S(2)}, u32[]{:S(2)}) collective-permute-start(bf16[48,768]{1,0:T(8,128)(2,1)S(1)} %get-tuple-element.23), channel_id=1, source_target_pairs={{0,2},{1,3},{2,0},{3,1},{4,6},{5,7},{6,4},{7,5},{8,10},{9,11},{10,... | collective-permute-start | bytes 221192 | tf_op jit(solution)/shard_map/ppermute | solution.py:21
  96.4 8.5 %collective-permute-start.18 = (bf16[48,768]{1,0:T(8,128)(2,1)S(1)}, bf16[48,768]{1,0:T(8,128)(2,1)S(1)}, u32[]{:S(2)}, u32[]{:S(2)}) collective-permute-start(bf16[48,768]{1,0:T(8,128)(2,1)S(1)} %get-tuple-element.23), channel_id=1, source_target_pairs={{0,3},{1,0},{2,1},{3,2},{4,7},{5,4},{6,5},{7,6},{8,11},{9,8},{10,9... | collective-permute-start | bytes 221192 | tf_op jit(solution)/shard_map/ppermute | solution.py:21
  104.9 10.2 %collective-permute-start.19 = (bf16[192,768]{1,0:T(8,128)(2,1)S(1)}, bf16[192,768]{1,0:T(8,128)(2,1)S(1)}, u32[]{:S(2)}, u32[]{:S(2)}) collective-permute-start(bf16[192,768]{1,0:T(8,128)(2,1)S(1)} %bitcast.196), channel_id=1, source_target_pairs={{0,4},{4,8},{8,12},{12,0},{1,5},{5,9},{9,13},{13,1},{2,6},{6,10},{... | collective-permute-start | bytes 884744 | tf_op jit(solution)/shard_map/ppermute | solution.py:21
  105.8 14.0 %collective-permute-start.20 = (bf16[192,768]{1,0:T(8,128)(2,1)S(1)}, bf16[192,768]{1,0:T(8,128)(2,1)S(1)}, u32[]{:S(2)}, u32[]{:S(2)}) collective-permute-start(bf16[192,768]{1,0:T(8,128)(2,1)S(1)} %bitcast.197), channel_id=1, source_target_pairs={{0,8},{4,12},{8,0},{12,4},{1,9},{5,13},{9,1},{13,5},{2,10},{6,14},... | collective-permute-start | bytes 884744 | tf_op jit(solution)/shard_map/ppermute | solution.py:21
  109.0 10.9 %collective-permute-start.21 = (bf16[192,768]{1,0:T(8,128)(2,1)S(1)}, bf16[192,768]{1,0:T(8,128)(2,1)S(1)}, u32[]{:S(2)}, u32[]{:S(2)}) collective-permute-start(bf16[192,768]{1,0:T(8,128)(2,1)S(1)} %bitcast.198), channel_id=1, source_target_pairs={{0,12},{4,0},{8,4},{12,8},{1,13},{5,1},{9,5},{13,9},{2,14},{6,2},{... | collective-permute-start | bytes 884744 | tf_op jit(solution)/shard_map/ppermute | solution.py:21
  144.8 8.6 %collective-permute-start.23 = (f32[2,96,256]{2,1,0:T(8,128)S(1)}, f32[2,96,256]{2,1,0:T(8,128)S(1)}, u32[]{:S(2)}, u32[]{:S(2)}) collective-permute-start(f32[2,96,256]{2,1,0:T(8,128)S(1)} %pad_maximum_fusion), channel_id=1, source_target_pairs={{0,32},{32,64},{64,96},{96,0},{1,33},{33,65},{65,97},{97,1},{2,34}... | collective-permute-start | bytes 589832 | tf_op jit(solution)/shard_map/ppermute | solution.py:21
  146.4 12.4 %collective-permute-start.24 = (f32[2,96,256]{2,1,0:T(8,128)S(1)}, f32[2,96,256]{2,1,0:T(8,128)S(1)}, u32[]{:S(2)}, u32[]{:S(2)}) collective-permute-start(f32[2,96,256]{2,1,0:T(8,128)S(1)} %pad_maximum_fusion.1), channel_id=1, source_target_pairs={{0,64},{32,96},{64,0},{96,32},{1,65},{33,97},{65,1},{97,33},{2,66}... | collective-permute-start | bytes 589832 | tf_op jit(solution)/shard_map/ppermute | solution.py:21
  149.4 9.4 %collective-permute-start.25 = (f32[2,96,256]{2,1,0:T(8,128)S(1)}, f32[2,96,256]{2,1,0:T(8,128)S(1)}, u32[]{:S(2)}, u32[]{:S(2)}) collective-permute-start(f32[2,96,256]{2,1,0:T(8,128)S(1)} %pad_maximum_fusion.2), channel_id=1, source_target_pairs={{0,96},{32,0},{64,32},{96,64},{1,97},{33,1},{65,33},{97,65},{2,98}... | collective-permute-start | bytes 589832 | tf_op jit(solution)/shard_map/ppermute | solution.py:21
  162.7 9.6 %collective-permute-start.29 = (bf16[2,96,256]{2,1,0:T(8,128)(2,1)S(1)}, bf16[2,96,256]{2,1,0:T(8,128)(2,1)S(1)}, u32[]{:S(2)}, u32[]{:S(2)}) collective-permute-start(bf16[2,96,256]{2,1,0:T(8,128)(2,1)S(1)} %pad_maximum_fusion.5), channel_id=1, source_target_pairs={{0,32},{32,64},{64,96},{96,0},{1,33},{33,65},{65,97},{97,1},{2,34}... | collective-permute-start | bytes 294920 | tf_op jit(solution)/shard_map/ppermute | solution.py:21
  177.6 9.8 %collective-permute-start.33 = (bf16[2,96,256]{2,1,0:T(8,128)(2,1)S(1)}, bf16[2,96,256]{2,1,0:T(8,128)(2,1)S(1)}, u32[]{:S(2)}, u32[]{:S(2)}) collective-permute-start(bf16[2,96,256]{2,1,0:T(8,128)(2,1)S(1)} %pad_maximum_fusion.8), channel_id=1, source_target_pairs={{0,96},{32,0},{64,32},{96,64},{1,97},{33,1},{65,33},{97,65},{2,98}... | collective-permute-start | bytes 294920 | tf_op jit(solution)/shard_map/ppermute | solution.py:21
  179.4 7.9 %collective-permute-start.31 = (bf16[2,96,256]{2,1,0:T(8,128)(2,1)S(1)}, bf16[2,96,256]{2,1,0:T(8,128)(2,1)S(1)}, u32[]{:S(2)}, u32[]{:S(2)}) collective-permute-start(bf16[2,96,256]{2,1,0:T(8,128)(2,1)S(1)} %pad_maximum_fusion.6), channel_id=1, source_target_pairs={{0,32},{32,64},{64,96},{96,0},{1,33},{33,65},{65,97},{97,1},{2,34}... | collective-permute-start | bytes 294920 | tf_op jit(solution)/shard_map/ppermute | solution.py:21
  179.8 7.6 %collective-permute-start.32 = (bf16[2,96,256]{2,1,0:T(8,128)(2,1)S(1)}, bf16[2,96,256]{2,1,0:T(8,128)(2,1)S(1)}, u32[]{:S(2)}, u32[]{:S(2)}) collective-permute-start(bf16[2,96,256]{2,1,0:T(8,128)(2,1)S(1)} %pad_maximum_fusion.7), channel_id=1, source_target_pairs={{0,64},{32,96},{64,0},{96,32},{1,65},{33,97},{65,1},{97,33},{2,66}... | collective-permute-start | bytes 294920 | tf_op jit(solution)/shard_map/ppermute | solution.py:21
  242.2 17.2 %collective-permute-start.44 = (f32[1]{0:T(128)}, f32[1]{0:T(128)}, u32[]{:S(2)}, u32[]{:S(2)}) collective-permute-start(f32[1]{0:T(128)} %bitcast.83), channel_id=1, source_target_pairs={{0,1},{1,2},{2,3},{3,0},{4,5},{5,6},{6,7},{7,4},{8,9},{9,10},{10,1... | collective-permute-start | bytes 20 | tf_op jit(solution)/shard_map/ppermute | solution.py:21
  243.6 17.1 %collective-permute-start.45 = (f32[1]{0:T(128)}, f32[1]{0:T(128)}, u32[]{:S(2)}, u32[]{:S(2)}) collective-permute-start(f32[1]{0:T(128)} %bitcast.83), channel_id=1, source_target_pairs={{0,2},{1,3},{2,0},{3,1},{4,6},{5,7},{6,4},{7,5},{8,10},{9,11},{10,... | collective-permute-start | bytes 20 | tf_op jit(solution)/shard_map/ppermute | solution.py:21
  246.3 15.1 %collective-permute-start.46 = (f32[1]{0:T(128)}, f32[1]{0:T(128)}, u32[]{:S(2)}, u32[]{:S(2)}) collective-permute-start(f32[1]{0:T(128)} %bitcast.83), channel_id=1, source_target_pairs={{0,3},{1,0},{2,1},{3,2},{4,7},{5,4},{6,5},{7,6},{8,11},{9,8},{10,9... | collective-permute-start | bytes 20 | tf_op jit(solution)/shard_map/ppermute | solution.py:21
  262.0 8.1 %collective-permute-start.47 = (f32[1]{0:T(128)}, f32[1]{0:T(128)}, u32[]{:S(2)}, u32[]{:S(2)}) collective-permute-start(f32[1]{0:T(128)} %add.406), channel_id=1, source_target_pairs={{0,4},{4,8},{8,12},{12,0},{1,5},{5,9},{9,13},{13,1},{2,6},{6,10},{... | collective-permute-start | bytes 20 | tf_op jit(solution)/shard_map/ppermute | solution.py:21
  273.9 9.7 %collective-permute-start.51 = (f32[1]{0:T(128)}, f32[1]{0:T(128)}, u32[]{:S(2)}, u32[]{:S(2)}) collective-permute-start(f32[1]{0:T(128)} %add.410), channel_id=1, source_target_pairs={{0,32},{32,64},{64,96},{96,0},{1,33},{33,65},{65,97},{97,1},{2,34}... | collective-permute-start | bytes 20 | tf_op jit(solution)/shard_map/ppermute | solution.py:21
  276.8 7.4 %collective-permute-start.52 = (f32[1]{0:T(128)}, f32[1]{0:T(128)}, u32[]{:S(2)}, u32[]{:S(2)}) collective-permute-start(f32[1]{0:T(128)} %add.410), channel_id=1, source_target_pairs={{0,64},{32,96},{64,0},{96,32},{1,65},{33,97},{65,1},{97,33},{2,66}... | collective-permute-start | bytes 20 | tf_op jit(solution)/shard_map/ppermute | solution.py:21
  (29 other events, 108.1 us)
Sparse Core Ops, SparseCore 0:
  21.9 119.7 reduce-scatter.1
  173.2 58.6 all-gather.1
